TPU v7x, 8 devices: a whole 2x2x1 slice. The times are simulated.
8 devices in a mesh: dp: 1 (over z), tp: 2 (over y), sq: 4 (over x, core).
Axes of the slice: x: 2, y: 2, z: 1, core: 2. Of those that a mesh axis runs over, the one named last changes fastest.
Arguments:
- hidden: bfloat16 [256, 4096], P('dp')
- cache_lens: int32 [256], P('dp')
- k_cache: bfloat16 [256, 1024, 128], P('dp', 'sq')
- v_cache: bfloat16 [256, 1024, 128], P('dp', 'sq')
- ln_gain: float32 [4096], replicated
- ln_bias: float32 [4096], replicated
- w_query: bfloat16 [4096, 4096], P(None, 'tp')
- b_query: float32 [4096], P('tp')
- w_kv: bfloat16 [4096, 256], replicated
- b_kv: float32 [256], replicated
- w_out: bfloat16 [4096, 4096], P('tp')
- b_out: float32 [4096], replicated
Outputs:
- output 1: bfloat16 [256, 4096], P('dp')
- output 2: bfloat16 [256, 1024, 128], P('dp', 'sq')
- output 3: bfloat16 [256, 1024, 128], P('dp', 'sq')
All inputs are finite; a program needn't handle non-finite values.
Results may differ from a plain program's by a relative error of at most 0.00346761.
Values sent between devices are 32-bit elements.
A program may use at most 1 GiB of HBM per device.

v0:
```python
import jax
import jax.numpy as jnp
from jax import lax
from jax.sharding import PartitionSpec as P


def layer_norm(x_rows, ln_gain, ln_bias):
    x_wide = x_rows.astype(jnp.float32)
    mean_val = jnp.mean(x_wide, axis=-1, keepdims=True)
    centered = x_wide - mean_val
    variance = jnp.mean(centered * centered, axis=-1, keepdims=True)
    normed = centered * lax.rsqrt(variance + 1e-5)
    return (normed * ln_gain + ln_bias).astype(jnp.bfloat16)


def solution(mesh):
    def local_step(hidden, cache_lens, k_cache, v_cache, ln_gain, ln_bias, w_query, b_query, w_kv, b_kv, w_out, b_out):
        batch, pos_local, head_dim = k_cache.shape
        heads_local = w_query.shape[1] // head_dim
        normed = layer_norm(hidden, ln_gain, ln_bias)
        query = (jnp.dot(normed, w_query, preferred_element_type=jnp.float32) + b_query).astype(jnp.bfloat16)
        query = query.reshape(batch, heads_local, head_dim)
        key_val = (jnp.dot(normed, w_kv, preferred_element_type=jnp.float32) + b_kv).astype(jnp.bfloat16)
        first_pos = lax.axis_index("sq") * pos_local
        positions = first_pos + lax.broadcasted_iota(jnp.int32, (1, pos_local), 1)
        at_slot = (positions == cache_lens[:, None])[:, :, None]
        key_new = jnp.where(at_slot, key_val[:, None, :head_dim], k_cache)
        val_new = jnp.where(at_slot, key_val[:, None, head_dim:], v_cache)
        scores = jnp.einsum("bnd,btd->bnt", query, key_new, preferred_element_type=jnp.float32) * (head_dim ** -0.5)
        valid = (positions <= cache_lens[:, None])[:, None, :]
        scores = jnp.where(valid, scores, -1e30)
        local_max = jnp.max(scores, axis=-1, keepdims=True)
        global_max = lax.pmax(local_max, "sq")
        weights = jnp.where(valid, jnp.exp(scores - global_max), 0.0)
        denominator = lax.psum(jnp.sum(weights, axis=-1, keepdims=True), "sq")
        numerator = lax.psum(jnp.einsum("bnt,btd->bnd", weights.astype(jnp.bfloat16), val_new, preferred_element_type=jnp.float32), "sq")
        attended = (numerator / denominator).astype(jnp.bfloat16).reshape(batch, heads_local * head_dim)
        part_sum = jnp.dot(attended, w_out, preferred_element_type=jnp.float32)
        projected = lax.psum(part_sum, "tp")
        out_hidden = (hidden.astype(jnp.float32) + projected + b_out).astype(jnp.bfloat16)
        return out_hidden, key_new, val_new

    cache_spec = P("dp", "sq", None)
    row_spec = P("dp", None)
    in_specs = (row_spec, P("dp"), cache_spec, cache_spec, P(None), P(None), P(None, "tp"), P("tp"), P(None, None), P(None), P("tp", None), P(None))
    out_specs = (row_spec, cache_spec, cache_spec)
    return jax.shard_map(local_step, mesh=mesh, in_specs=in_specs, out_specs=out_specs, check_vma=False)
```

profile of v0, /device:TPU:0, one launch (start us, length us, event | category | flops | bytes accessed | tf_op | source)
XLA Modules:
  0.0 253.3 jit_solution(14908098689492022204)
XLA Ops:
  7.2 0.0 copy-start
  7.2 0.0 all-reduce.3.cloned.1.call-start
  7.3 2.1 convert_reduce_fusion
  9.4 2.3 fusion.2
  11.8 0.9 fusion.20
  12.8 8.5 %fusion.19 = bf16[32,8,16,128]{3,1,2,0:T(8,128)(2,1)S(1)} fusion(bf16[4096,2048]{1,0:T(8,128)(2,1)} %param.18, f32[2048]{0:T(1024)S(1)} %copy-done.7, bf16[256,4096]{1,0:T(8,128)(2,1)S(1)} %copy-done.2, f32[4096]{0:T(1024)S(1)} %copy-done.5, f32[4096]{0:T(1024)S(1)} %copy-done.6, f32[256]{0:T(256)S(1)} %add_rsqrt_fusion, f32[256]{0:T(256)S(1)} %broadcast_multiply_fusion), kind=kOutput, calls=%fused_computation.27 | convolution fusion | flops 4302307328 | bytes 19965952 | tf_op jit(solution)/shard_map/dot_general | solution.py:21
  21.3 0.2 copy.15
  21.6 0.1 broadcast_compare_fusion.1
  21.7 0.4 slice-done.2
  22.2 1.2 slice-done.3
  23.4 17.4 %broadcast_select_fusion.1 = (bf16[256,256,128]{2,1,0:T(8,128)(2,1)}, bf16[256,256,128]{2,1,0:T(8,128)(2,1)}) fusion(bf16[256,256,128]{2,1,0:T(8,128)(2,1)S(1)} %bitcast.14, pred[256,256]{1,0:T(8,128)(4,1)S(1)} %get-tuple-element.8, bf16[256,128]{1,0:T(8,128)(2,1)S(1)} %get-tuple-element.3, bf16[256,256,128]{2,1,0:T(8,128)(2,1)} %param.15, ...), kind=kLoop, calls=%fused_computation.1 | loop fusion | flops 16777216 | bytes 67305472 | tf_op jit(solution)/shard_map/jit(_where)/select_n | solution.py:27
  40.8 12.2 %fusion.8 = (f32[256,16]{1,0:T(8,128)S(1)}, f32[256,16,256]{2,1,0:T(8,128)}) fusion(pred[256,256]{1,0:T(8,128)(4,1)S(1)} %get-tuple-element.7, bf16[256,16,128]{2,1,0:T(8,128)(2,1)S(1)} %bitcast.15, bf16[256,256,128]{2,1,0:T(8,128)(2,1)} %get-tuple-element.5), kind=kOutput, calls=%fused_computation.15 | convolution fusion | flops 271577088 | bytes 22102016 | tf_op jit(solution)/shard_map/bnd,btd->bnt/dot_general | solution.py:29
  53.0 14.8 %pmax.7 = f32[256,16]{1,0:T(8,128)S(1)} all-reduce(f32[256,16]{1,0:T(8,128)S(1)} %get-tuple-element.9), channel_id=1, replica_groups=mesh['dp'=1,'tp'=2,'sq'=4] {'sq'}, use_global_device_ids=true, to_apply=%region_3.4 | all-reduce | flops 4096 | bytes 32768 | tf_op jit(solution)/shard_map/pmax | solution.py:33
  67.8 11.2 %fusion.12 = f32[256,16,128]{2,1,0:T(8,128)} fusion(bf16[256,256,128]{2,1,0:T(8,128)(2,1)} %get-tuple-element.6, f32[256,16,256]{2,1,0:T(8,128)} %get-tuple-element.10, f32[256,16]{1,0:T(8,128)S(1)} %pmax.7, pred[256,256]{1,0:T(8,128)(4,1)S(1)} %get-tuple-element.7), kind=kOutput, calls=%fused_computation.20 | convolution fusion | flops 273678336 | bytes 23150592 | tf_op jit(solution)/shard_map/bnt,btd->bnd/dot_general | solution.py:36
  79.0 0.0 all-reduce.3.cloned.1.call-update
  79.0 0.0 all-reduce.5.cloned.1.call-start
  79.1 3.6 %fusion.9 = f32[256,16]{1,0:T(8,128)S(1)} fusion(f32[256,16,256]{2,1,0:T(8,128)} %get-tuple-element.10, f32[256,16]{1,0:T(8,128)S(1)} %pmax.7, pred[256,256]{1,0:T(8,128)(4,1)S(1)} %get-tuple-element.7), kind=kLoop, calls=%fused_computation.16 | loop fusion | flops 5238784 | bytes 4292608 | tf_op jit(solution)/shard_map/reduce_sum | solution.py:35
  82.7 15.2 %psum.22 = f32[256,16]{1,0:T(8,128)S(1)} all-reduce(f32[256,16]{1,0:T(8,128)S(1)} %fusion.9), channel_id=1, replica_groups=mesh['dp'=1,'tp'=2,'sq'=4] {'sq'}, use_global_device_ids=true, to_apply=%region_6.7 | all-reduce | flops 4096 | bytes 32768 | tf_op jit(solution)/shard_map/psum | solution.py:35
  97.9 29.1 %all-reduce.3.cloned.1.call-done = f32[256,16,128]{2,1,0:T(8,128)} async-done(((f32[256,16,128]{2,1,0:T(8,128)}), f32[256,16,128]{2,1,0:T(8,128)}) %all-reduce.3.cloned.1.call-update) | async-done | bytes 2097168 | tf_op jit(solution)/shard_map/psum | solution.py:36
  127.0 1.9 divide_convert_fusion
  128.9 10.4 %fusion.21 = f32[256,4096]{1,0:T(8,128)} fusion(bf16[2048,4096]{1,0:T(8,128)(2,1)} %param.22, bf16[32,8,16,128]{3,2,1,0:T(8,128)(2,1)S(1)} %bitcast.16), kind=kOutput, calls=%fused_computation.30 | convolution fusion | flops 4294967296 | bytes 22020096 | tf_op jit(solution)/shard_map/dot_general | solution.py:38
  139.3 0.0 all-reduce.5.cloned.1.call-update
  139.4 102.3 %all-reduce.5.cloned.1.call-done = f32[256,4096]{1,0:T(8,128)} async-done(((f32[256,4096]{1,0:T(8,128)}), f32[256,4096]{1,0:T(8,128)}) %all-reduce.5.cloned.1.call-update) | async-done | bytes 4194320 | tf_op jit(solution)/shard_map/psum | solution.py:39
  241.7 4.8 %fusion.7 = bf16[256,4096]{1,0:T(8,128)(2,1)} fusion(f32[256,4096]{1,0:T(8,128)} %all-reduce.5.cloned.1.call-done, bf16[256,4096]{1,0:T(8,128)(2,1)} %param.12, f32[4096]{0:T(1024)S(1)} %copy-done.3), kind=kLoop, calls=%fused_computation.12 | loop fusion | flops 4194304 | bytes 8404992 | tf_op jit(solution)/shard_map/convert_element_type | solution.py:40
  (28 shorter events, 0.1 us)
Async XLA Ops:
  7.2 4.5 %copy-start = (bf16[4096,256]{1,0:T(8,128)(2,1)S(1)}, bf16[4096,256]{1,0:T(8,128)(2,1)}, u32[]{:S(2)}) copy-start(bf16[4096,256]{1,0:T(8,128)(2,1)} %param.20) | copy-start | bytes 6291460
  7.2 4.5 %copy-start.5 = (f32[4096]{0:T(1024)S(1)}, f32[4096]{0:T(1024)}, u32[]{:S(2)}) copy-start(f32[4096]{0:T(1024)} %param.17) | copy-start | bytes 49156
  7.2 4.5 %copy-start.6 = (f32[4096]{0:T(1024)S(1)}, f32[4096]{0:T(1024)}, u32[]{:S(2)}) copy-start(f32[4096]{0:T(1024)} %param.16) | copy-start | bytes 49156
  7.2 4.5 %copy-start.8 = (f32[256]{0:T(256)S(1)}, f32[256]{0:T(256)}, u32[]{:S(2)}) copy-start(f32[256]{0:T(256)} %param.21) | copy-start | bytes 3076
  7.2 119.8 %all-reduce.3.cloned.1.call-start = ((), (), s32[]{:S(2)}) async-start(), calls=%async_computation | async-start | bytes 4194304 | tf_op jit(solution)/shard_map/psum | solution.py:36
  7.3 4.5 %copy-start.2 = (bf16[256,4096]{1,0:T(8,128)(2,1)S(1)}, bf16[256,4096]{1,0:T(8,128)(2,1)}, u32[]{:S(2)}) copy-start(bf16[256,4096]{1,0:T(8,128)(2,1)} %param.12) | copy-start | bytes 6291460
  11.7 1.0 copy-start.7
  12.7 9.0 %slice-start = ((s8[16777216]{0:T(1024)(128)(4,1)}), s8[4194304]{0:T(1024)(128)(4,1)S(1)}, s32[]{:S(2)}) async-start(s8[16777216]{0:T(1024)(128)(4,1)} %bitcast.13), calls=%async_computation.2 | async-start | bytes 8388608
  12.7 8.8 %copy-start.4 = (s32[256]{0:T(256)S(1)}, s32[256]{0:T(256)}, u32[]{:S(2)}) copy-start(s32[256]{0:T(256)} %param.13) | copy-start | bytes 3076
  12.8 9.0 %slice-start.1 = ((s8[16777216]{0:T(1024)(128)(4,1)}), s8[4194304]{0:T(1024)(128)(4,1)S(1)}, s32[]{:S(2)}) async-start(s8[16777216]{0:T(1024)(128)(4,1)} %bitcast.13), calls=%async_computation.3 | async-start | bytes 8388608
  12.8 9.4 %slice-start.2 = ((s8[16777216]{0:T(1024)(128)(4,1)}), s8[4194304]{0:T(1024)(128)(4,1)S(1)}, s32[]{:S(2)}) async-start(s8[16777216]{0:T(1024)(128)(4,1)} %bitcast.13), calls=%async_computation.4 | async-start | bytes 8388608
  12.8 10.6 %slice-start.3 = ((s8[16777216]{0:T(1024)(128)(4,1)}), s8[4194304]{0:T(1024)(128)(4,1)S(1)}, s32[]{:S(2)}) async-start(s8[16777216]{0:T(1024)(128)(4,1)} %bitcast.13), calls=%async_computation.5 | async-start | bytes 8388608
  79.0 162.6 %all-reduce.5.cloned.1.call-start = ((), (), s32[]{:S(2)}) async-start(), calls=%async_computation.1 | async-start | bytes 8388608 | tf_op jit(solution)/shard_map/psum | solution.py:39
  139.3 102.3 %copy-start.3 = (f32[4096]{0:T(1024)S(1)}, f32[4096]{0:T(1024)}, u32[]{:S(2)}) copy-start(f32[4096]{0:T(1024)} %param.23) | copy-start | bytes 49156
  139.3 107.1 %copy-start.1 = (bf16[4096,256]{1,0:T(8,128)(2,1)S(1)}, bf16[4096,256]{1,0:T(8,128)(2,1)}, u32[]{:S(2)}) copy-start(bf16[4096,256]{1,0:T(8,128)(2,1)} %param.20) | copy-start | bytes 6291460
Sparse Core Ops, SparseCore 0:
  79.1 47.8 all-reduce.2
  139.5 102.1 all-reduce.4
where the time goes:
time: 254 us; the launch traced here: 253 us
  waiting for transfers between devices  131 us (52%)
  matrix products  43.2 us (17%)
  other arithmetic  32.3 us (13%)
  blocking collectives  30 us (12%)
  between operations  14.3 us (6%)
    psum x1, waiting for transfers between devices, local_step(): projected = lax.psum(part_sum, 'tp')  102 us
    psum x1, waiting for transfers between devices, local_step(): lax.psum(jnp.einsum('bnt,btd->bnd', weights.astype(jnp.bfloat16), val_new...  29.1 us
    select_n x1, other arithmetic, local_step(): key_new = jnp.where(at_slot, key_val[:, None, :head_dim], k_cache)  17.4 us
    psum x1, blocking collectives, local_step(): denominator = lax.psum(jnp.sum(weights, axis=-1, keepdims=True), 'sq')  15.2 us
    pmax x1, blocking collectives, local_step(): global_max = lax.pmax(local_max, 'sq')  14.8 us
    dot_general x1, matrix products, local_step(): jnp.einsum('bnd,btd->bnt', query, key_new, preferred_element_type=jnp.flo...  12.2 us
    dot_general x1, matrix products, local_step(): jnp.einsum('bnt,btd->bnd', weights.astype(jnp.bfloat16), val_new, preferr...  11.2 us
    dot_general x1, matrix products, local_step(): part_sum = jnp.dot(attended, w_out, preferred_element_type=jnp.float32)  10.4 us
  transfers between devices with their start and end apart: 2, of which 2 were waited for; matrix products, arithmetic and copies ran while one was open for 1% of the time, Pallas kernels for 0%

commit v1 on v0

v1 whole, which is shorter than its diff:
```python
import functools
import math

import jax
import jax.numpy as jnp
from jax import lax
from jax.experimental import pallas as pl
from jax.experimental.pallas import tpu as pltpu
from jax.sharding import PartitionSpec as P

MESH = pl.DeviceIdType.MESH
F32 = jnp.float32
BF16 = jnp.bfloat16
NEG = -1e30
B = 256
D = 4096
H = 16
DH = 128
T = 256
NC = 4
CS = B // NC
S = CS // 4
HALF = S // 2
QB = 512
NQ = H * DH // QB
QSCALE = DH ** -0.5 * math.log2(math.e)
GROUP = 8
MIB = 1024 * 1024


def attention_kernel(lens, hid_hbm, k_hbm, v_hbm, gain_ref, bias_ref, wq_hbm, bq_ref, wkv_hbm, bkv_ref,
                     o_ref, lse_ref, ko_hbm, vo_hbm,
                     hid, h, wq, wkv, q3, kv, kbuf, vbuf, wsem, ksem, vsem, osem):
    first = lax.axis_index("sq") * T
    load_h = pltpu.make_async_copy(hid_hbm, hid, wsem.at[NQ])
    load_h.start()
    load_wq = []
    for j in range(NQ):
        cols = pl.ds(j * QB, QB)
        load_wq.append(pltpu.make_async_copy(wq_hbm.at[:, cols], wq.at[:, cols], wsem.at[j]))
    load_wkv = pltpu.make_async_copy(wkv_hbm, wkv, wsem.at[NQ + 1])
    load_wkv.start()
    for c in load_wq:
        c.start()
    load_k, load_v = [], []
    for k in range(NC):
        rows = pl.ds(k * CS, CS)
        load_k.append(pltpu.make_async_copy(k_hbm.at[rows], kbuf.at[rows], ksem.at[k]))
        load_v.append(pltpu.make_async_copy(v_hbm.at[rows], vbuf.at[rows], vsem.at[k]))
        load_k[-1].start()
        load_v[-1].start()
    load_h.wait()

    def norm_rows(i, _):
        rows = pl.ds(pl.multiple_of(i * 16, 16), 16)
        x = hid[rows, :].astype(F32)
        mean = jnp.sum(x, axis=-1, keepdims=True) * (1.0 / D)
        cen = x - mean
        var = jnp.sum(cen * cen, axis=-1, keepdims=True) * (1.0 / D)
        y = cen * lax.rsqrt(var + 1e-5)
        h[rows, :] = (y * gain_ref[...] + bias_ref[...]).astype(BF16)
        return 0

    lax.fori_loop(0, B // 16, norm_rows, 0, unroll=2)
    load_wkv.wait()
    new_kv = (jnp.dot(h[...], wkv[...], preferred_element_type=F32) + bkv_ref[...]).astype(BF16).astype(F32)
    kv[0:B, :] = new_kv[:, :DH]
    kv[B:2 * B, :] = new_kv[:, DH:]
    for j in range(NQ):
        load_wq[j].wait()
        cols = pl.ds(j * QB, QB)
        q = jnp.dot(h[...], wq[:, cols], preferred_element_type=F32) + bq_ref[:, cols]
        q = q.astype(BF16).astype(F32)
        for n in range(QB // DH):
            q3[pl.ds(j * (QB // DH) + n, B, stride=H), :] = q[:, n * DH:(n + 1) * DH]

    sub = lax.broadcasted_iota(jnp.int32, (16, DH), 0)
    lane = lax.broadcasted_iota(jnp.int32, (H, DH), 1)
    pos = lax.broadcasted_iota(jnp.int32, (H, T), 1)
    zero = jnp.zeros((H, DH), BF16)

    def insert(b, _):
        row = lens[b] - first
        start = pl.multiple_of((jnp.clip(row, 0, T - 1) // 16) * 16, 16)
        hit = sub == row - start
        for buf, c in ((kbuf, 0), (vbuf, 1)):
            new = kv[pl.ds(c * B + b, 1), :]
            old = buf[b, pl.ds(start, 16), :].astype(F32)
            buf[b, pl.ds(start, 16), :] = jnp.where(hit, new, old).astype(BF16)
        return 0

    def attend(i, k):
        base = i * GROUP
        lses = lse_ref[pl.ds(k * H, H), :]
        for u in range(0, GROUP, 2):
            b = base + u
            q0 = q3[pl.ds(pl.multiple_of(b * H, H), H), :].astype(BF16)
            q1 = q3[pl.ds(pl.multiple_of(b * H + H, H), H), :].astype(BF16)
            lhs = jnp.concatenate([jnp.concatenate([q0, zero], 1), jnp.concatenate([zero, q1], 1)], 0)
            keys = jnp.concatenate([kbuf[b], kbuf[b + 1]], 1)
            vals = jnp.concatenate([vbuf[b], vbuf[b + 1]], 1)
            s = lax.dot_general(lhs, keys, (((1,), (1,)), ((), ())), preferred_element_type=F32)
            ps, ls, ms = [], [], []
            for e in range(2):
                se = jnp.where(pos <= lens[b + e] - first, s[e * H:(e + 1) * H] * QSCALE, NEG)
                m = jnp.max(se, axis=1, keepdims=True)
                p = jnp.exp2(se - m)
                ps.append(p)
                ms.append(m)
                ls.append(jnp.sum(p, axis=1, keepdims=True))
            o = jnp.dot(jnp.concatenate(ps, 0).astype(BF16), vals, preferred_element_type=F32)
            for e in range(2):
                o_ref[pl.ds(pl.multiple_of((b + e) * H, H), H), :] = o[e * H:(e + 1) * H, e * DH:(e + 1) * DH] / ls[e]
                lses = jnp.where(lane == b + e - k * CS, ms[e] + jnp.log2(ls[e]), lses)
        lse_ref[pl.ds(k * H, H), :] = lses
        return k

    stores = []
    for k in range(NC):
        load_k[k].wait()
        load_v[k].wait()
        lse_ref[pl.ds(k * H, H), :] = jnp.zeros((H, DH), F32)
        lax.fori_loop(k * CS, (k + 1) * CS, insert, 0, unroll=4)
        lax.fori_loop(k * CS // GROUP, (k + 1) * CS // GROUP, lambda i, c, k=k: attend(i, k), k)
        rows = pl.ds(k * CS, CS)
        for e, (buf, out) in enumerate(((kbuf, ko_hbm), (vbuf, vo_hbm))):
            st = pltpu.make_async_copy(buf.at[rows], out.at[rows], osem.at[2 * k + e])
            st.start()
            stores.append(st)
    for st in stores:
        st.wait()


def column(tile, j):
    return tile[:, j:j + 1]


def merge(la, lb):
    top = jnp.maximum(la, lb)
    wa, wb = jnp.exp2(la - top), jnp.exp2(lb - top)
    tot = wa + wb
    return wa / tot, wb / tot, top + jnp.log2(tot)


def combine_kernel(o_ref, lse_ref, wo_hbm, y_ref,
                   wo, o_core, l_core, o_mix, l_mix, o_x, l_x, a3, part, p_y,
                   wsem, a0s, a0r, a1s, a1r, bs, br, cs, cr, ds, dr):
    sq, tp = lax.axis_index("sq"), lax.axis_index("tp")
    x, c = sq // 2, sq % 2
    mate = {"sq": x * 2 + 1 - c}
    over_x = {"sq": (1 - x) * 2 + c}
    over_y = {"tp": 1 - tp}
    load = pltpu.make_async_copy(wo_hbm, wo, wsem)
    load.start()
    bar = pltpu.get_barrier_semaphore()
    for dev in (mate, over_x, over_y):
        pl.semaphore_signal(bar, inc=1, device_id=dev, device_id_type=MESH)
    pl.semaphore_wait(bar, 3)

    def send(src, dst, ssem, rsem, dev):
        cp = pltpu.make_async_remote_copy(src, dst, ssem, rsem, device_id=dev, device_id_type=MESH)
        cp.start()
        return cp

    W = 2 * S * H
    sent = []
    hop0, hop1, hopb, hopc, hopd = [], [], [], [], []
    for k in range(NC):
        other = pl.multiple_of(k * CS * H + (1 - c) * W, W)
        hop0.append((send(o_ref.at[pl.ds(other, W)], o_core.at[k], a0s.at[k, 0], a0r.at[k, 0], mate),
                     send(lse_ref.at[pl.ds(k * H, H)], l_core.at[k], a0s.at[k, 1], a0r.at[k, 1], mate)))
    for k in range(NC):
        for cp in hop0[k]:
            cp.wait_recv()
        shift = lax.rem(DH - c * 2 * S, DH)
        fa, fb, lm = merge(pltpu.roll(lse_ref[pl.ds(k * H, H), :], shift, 1), pltpu.roll(l_core[k], shift, 1))
        l_mix[k] = lm
        mine = k * CS * H + c * W
        for j in range(2 * S):
            oa = o_ref[pl.ds(pl.multiple_of(mine + j * H, H), H), :]
            ob = o_core[k, j * H:(j + 1) * H, :]
            o_mix[k, j * H:(j + 1) * H, :] = column(fa, j) * oa + column(fb, j) * ob
        far = pl.multiple_of((1 - x) * S * H, S * H)
        hop1.append((send(o_mix.at[k, pl.ds(far, S * H)], o_x.at[k], a1s.at[k, 0], a1r.at[k, 0], over_x),
                     send(l_mix.at[k], l_x.at[k], a1s.at[k, 1], a1r.at[k, 1], over_x)))

    def project(k):
        for cp in hop1[k]:
            cp.wait_recv()
        shift = lax.rem(DH - x * S, DH)
        fa, fb, _ = merge(pltpu.roll(l_mix[k], shift, 1), pltpu.roll(l_x[k], shift, 1))
        near = x * S * H
        for j in range(S):
            oa = o_mix[k, pl.ds(pl.multiple_of(near + j * H, H), H), :]
            ob = o_x[k, j * H:(j + 1) * H, :]
            a3[j * H:(j + 1) * H, :] = column(fa, j) * oa + column(fb, j) * ob
        a = jnp.concatenate([a3[pl.ds(n, S, stride=H), :].astype(BF16) for n in range(H)], 1)
        if k == 0:
            load.wait()

        def cols(i, _):
            cc = pl.ds(pl.multiple_of(i * 1024, 1024), 1024)
            part[k, :, cc] = jnp.dot(a, wo[:, cc], preferred_element_type=F32)
            return 0

        lax.fori_loop(0, D // 1024, cols, 0)
        far = pl.multiple_of((1 - tp) * HALF, HALF)
        hopb.append(send(part.at[k, pl.ds(far, HALF)], p_y.at[k], bs.at[k], br.at[k], over_y))

    def rows_of(k, xx, yy):
        return pl.ds(pl.multiple_of(k * CS + (c * 2 + xx) * S + yy * HALF, HALF), HALF)

    def finish(k):
        hopb[k].wait_recv()
        rows = rows_of(k, x, tp)
        y_ref[rows, :] = part[k, pl.ds(pl.multiple_of(tp * HALF, HALF), HALF), :] + p_y[k]
        hopc.append((send(y_ref.at[rows], y_ref.at[rows], cs.at[k, 0], cr.at[k, 0], over_x),
                     send(y_ref.at[rows], y_ref.at[rows], cs.at[k, 1], cr.at[k, 1], over_y)))
        hopd.append([send(y_ref.at[rows], y_ref.at[rows], ds.at[k, 0], dr.at[k, 0], mate)])

    def relay(k):
        hopc[k][0].wait_recv()
        rows, lo, hi = rows_of(k, 1 - x, tp), pl.ds(0, D // 2), pl.ds(D // 2, D // 2)
        d1 = send(y_ref.at[rows, lo], y_ref.at[rows, lo], cs.at[k, 2], cr.at[k, 2], over_y)
        hopd[k].append(send(y_ref.at[rows], y_ref.at[rows], ds.at[k, 1], dr.at[k, 1], mate))
        hopc[k][1].wait_recv()
        rows = rows_of(k, x, 1 - tp)
        d2 = send(y_ref.at[rows, hi], y_ref.at[rows, hi], cs.at[k, 3], cr.at[k, 3], over_x)
        hopd[k].append(send(y_ref.at[rows], y_ref.at[rows], ds.at[k, 2], dr.at[k, 2], mate))
        hopc[k] = hopc[k] + (d1, d2)

    def last(k):
        hopc[k][2].wait_recv()
        hopc[k][3].wait_recv()
        rows = rows_of(k, 1 - x, 1 - tp)
        hopd[k].append(send(y_ref.at[rows], y_ref.at[rows], ds.at[k, 3], dr.at[k, 3], mate))

    for step in range(NC + 3):
        if step < NC:
            project(step)
        if 0 <= step - 1 < NC:
            finish(step - 1)
        if 0 <= step - 2 < NC:
            relay(step - 2)
        if 0 <= step - 3 < NC:
            last(step - 3)
    for k in range(NC):
        for cp in hopd[k]:
            cp.wait_recv()
    for k in range(NC):
        for cp in hop0[k] + hop1[k] + (hopb[k],) + hopc[k] + tuple(hopd[k]):
            cp.wait_send()


def solution(mesh):
    def local_step(hidden, cache_lens, k_cache, v_cache, ln_gain, ln_bias, w_query, b_query, w_kv, b_kv, w_out, b_out):
        hbm = pl.BlockSpec(memory_space=pltpu.HBM)
        vm = pl.BlockSpec(memory_space=pltpu.VMEM)
        cache = jax.ShapeDtypeStruct((B, T, DH), BF16)
        o, lse, k_new, v_new = pl.pallas_call(
            attention_kernel,
            out_shape=(pltpu.VMEM((B * H, DH), F32), pltpu.VMEM((NC * H, DH), F32), cache, cache),
            in_specs=[pl.BlockSpec(memory_space=pltpu.SMEM), hbm, hbm, hbm, vm, vm, hbm, vm, hbm, vm],
            out_specs=(vm, vm, hbm, hbm),
            scratch_shapes=[
                pltpu.VMEM((B, D), BF16), pltpu.VMEM((B, D), BF16), pltpu.VMEM((D, H * DH), BF16), pltpu.VMEM((D, 2 * DH), BF16),
                pltpu.VMEM((B * H, DH), F32), pltpu.VMEM((2 * B, DH), F32),
                pltpu.VMEM((B, T, DH), BF16), pltpu.VMEM((B, T, DH), BF16),
                pltpu.SemaphoreType.DMA((NQ + 2,)), pltpu.SemaphoreType.DMA((NC,)), pltpu.SemaphoreType.DMA((NC,)),
                pltpu.SemaphoreType.DMA((2 * NC,)),
            ],
            compiler_params=pltpu.CompilerParams(vmem_limit_bytes=60 * MIB),
            name="attention",
        )(cache_lens, hidden, k_cache, v_cache, ln_gain[None], ln_bias[None], w_query, b_query[None], w_kv, b_kv[None])
        sem = pltpu.SemaphoreType.DMA
        y = pl.pallas_call(
            combine_kernel,
            out_shape=pltpu.VMEM((B, D), F32),
            in_specs=[vm, vm, hbm],
            out_specs=vm,
            scratch_shapes=[
                pltpu.VMEM((H * DH, D), BF16),
                pltpu.VMEM((NC, 2 * S * H, DH), F32), pltpu.VMEM((NC, H, DH), F32),
                pltpu.VMEM((NC, 2 * S * H, DH), F32), pltpu.VMEM((NC, H, DH), F32),
                pltpu.VMEM((NC, S * H, DH), F32), pltpu.VMEM((NC, H, DH), F32),
                pltpu.VMEM((S * H, DH), F32),
                pltpu.VMEM((NC, S, D), F32), pltpu.VMEM((NC, HALF, D), F32),
                sem, sem((NC, 2)), sem((NC, 2)), sem((NC, 2)), sem((NC, 2)), sem((NC,)), sem((NC,)),
                sem((NC, 4)), sem((NC, 4)), sem((NC, 4)), sem((NC, 4)),
            ],
            compiler_params=pltpu.CompilerParams(vmem_limit_bytes=36 * MIB, collective_id=0, has_side_effects=True),
            name="combine",
        )(o, lse, w_out)
        out_hidden = (hidden.astype(F32) + y + b_out).astype(BF16)
        return out_hidden, k_new, v_new

    cache_spec = P("dp", "sq", None)
    row_spec = P("dp", None)
    in_specs = (row_spec, P("dp"), cache_spec, cache_spec, P(None), P(None), P(None, "tp"), P("tp"), P(None, None), P(None), P("tp", None), P(None))
    out_specs = (row_spec, cache_spec, cache_spec)
    return jax.shard_map(local_step, mesh=mesh, in_specs=in_specs, out_specs=out_specs, check_vma=False)
```

time: 254 us -> 109 us (0.43)
  waiting for transfers between devices: 131 us -> 0 us
  Pallas kernels: 0 us -> 106 us
  matrix products: 43.2 us -> 0 us
  other arithmetic: 32.3 us -> 1.93 us
  blocking collectives: 30 us -> 0 us
  between operations: 14.3 us -> 0.68 us
    psum x2 -> x0, waiting for transfers between devices: 131 us -> none  [the longest x1 102 us: local_step(): projected = lax.psum(part_sum, 'tp')]
    pallas_call x0 -> x2, Pallas kernels: none -> 106 us  [the longest x1 60.3 us: local_step(): pl.pallas_call(attention_kernel, out_shape=(pltpu.VMEM((B * H, DH), F32),...]
    dot_general x5 -> x0, matrix products: 43.2 us -> none  [the longest x1 12.2 us: local_step(): jnp.einsum('bnd,btd->bnt', query, key_new, preferred_element_type=jnp.flo...]
    select_n x1 -> x0, other arithmetic: 17.4 us -> none  [local_step(): key_new = jnp.where(at_slot, key_val[:, None, :head_dim], k_cache)]
    psum x1 -> x0, blocking collectives: 15.2 us -> none  [local_step(): denominator = lax.psum(jnp.sum(weights, axis=-1, keepdims=True), 'sq')]
    pmax x1 -> x0, blocking collectives: 14.8 us -> none  [local_step(): global_max = lax.pmax(local_max, 'sq')]
    reduce_sum x3 -> x0, other arithmetic: 8.02 us -> none  [the longest x1 3.63 us: local_step(): denominator = lax.psum(jnp.sum(weights, axis=-1, keepdims=True), 'sq')]
    convert_element_type x2 -> x1, other arithmetic: 6.74 us -> 1.93 us  [local_step(): out_hidden = (hidden.astype(F32) + y + b_out).astype(BF16)]
  transfers between devices with their start and end apart: 2 -> 0, of which waited for: 2 -> 0; matrix products, arithmetic and copies ran while one was open for 1% -> 0% of each run, Pallas kernels for 0% -> 0%
where the time goes in v1:
time: 109 us
  Pallas kernels  106 us (97%)
  other arithmetic  1.93 us (2%)
    pallas_call x1, Pallas kernels, local_step(): pl.pallas_call(attention_kernel, out_shape=(pltpu.VMEM((B * H, DH), F32),...  60.3 us
    pallas_call x1, Pallas kernels, local_step(): pl.pallas_call(combine_kernel, out_shape=pltpu.VMEM((B, D), F32), in_spec...  46.2 us

profile of v1, /device:TPU:0, one launch (start us, length us, event | category | flops | bytes accessed | tf_op | source)
XLA Modules:
  0.0 109.1 jit_solution(14915720017500494748)
XLA Ops:
  0.6 60.3 %attention.1 = (f32[4096,128]{1,0:T(8,128)S(1)}, f32[64,128]{1,0:T(8,128)S(1)}, bf16[256,256,128]{2,1,0:T(8,128)(2,1)}, bf16[256,256,128]{2,1,0:T(8,128)(2,1)}) custom-call(s32[256]{0:T(256)} %lens.1, bf16[256,4096]{1,0:T(8,128)(2,1)} %hid_hbm.1, bf16[256,256,128]{2,1,0:T(8,128)(2,1)} %k_hbm.1, bf16[256,256,128]{2,1,0:T(8,128)(2,1)} %v_hbm.1, ...), custom_call_target="tpu_custom_call" | custom-call | tf_op jit(solution)/shard_map/attention/pallas_call | solution.py:260
  60.9 0.0 copy-start
  60.9 0.0 copy-start.1
  60.9 46.2 %combine.1 = f32[256,4096]{1,0:T(8,128)S(1)} custom-call(f32[4096,128]{1,0:T(8,128)S(1)} %get-tuple-element.7.o_ref, f32[64,128]{1,0:T(8,128)S(1)} %get-tuple-element.8.lse_ref, bf16[2048,4096]{1,0:T(8,128)(2,1)} %wo_hbm.1), custom_call_target="tpu_custom_call" | custom-call | tf_op jit(solution)/shard_map/combine/pallas_call | solution.py:276
  107.1 0.0 copy-done
  107.1 0.0 copy-done.1
  107.1 1.9 %add_convert_fusion = bf16[256,4096]{1,0:T(8,128)(2,1)} fusion(f32[256,4096]{1,0:T(8,128)S(1)} %combine.1, bf16[256,4096]{1,0:T(8,128)(2,1)S(1)} %copy-done, f32[4096]{0:T(1024)S(1)} %copy-done.1), kind=kLoop, calls=%fused_computation | loop fusion | flops 4194304 | bytes 8404992 | tf_op jit(solution)/shard_map/convert_element_type | solution.py:294
Async XLA Ops:
  60.9 46.2 %copy-start = (bf16[256,4096]{1,0:T(8,128)(2,1)S(1)}, bf16[256,4096]{1,0:T(8,128)(2,1)}, u32[]{:S(2)}) copy-start(bf16[256,4096]{1,0:T(8,128)(2,1)} %hid_hbm.1) | copy-start | bytes 6291460
  60.9 46.2 %copy-start.1 = (f32[4096]{0:T(1024)S(1)}, f32[4096]{0:T(1024)}, u32[]{:S(2)}) copy-start(f32[4096]{0:T(1024)} %param.23) | copy-start | bytes 49156

commit v2 on v1

--- a/solution.py
+++ b/solution.py
@@ -30,7 +30,7 @@
 
 def attention_kernel(lens, hid_hbm, k_hbm, v_hbm, gain_ref, bias_ref, wq_hbm, bq_ref, wkv_hbm, bkv_ref,
                      o_ref, lse_ref, ko_hbm, vo_hbm,
-                     hid, h, wq, wkv, q3, kv, kbuf, vbuf, wsem, ksem, vsem, osem):
+                     hid, h, wq, wkv, q3, kv, kbuf, vbuf, s_a, s_b, p_a, p_b, wsem, ksem, vsem, osem):
     first = lax.axis_index("sq") * T
     load_h = pltpu.make_async_copy(hid_hbm, hid, wsem.at[NQ])
     load_h.start()
@@ -89,31 +89,55 @@
             buf[b, pl.ds(start, 16), :] = jnp.where(hit, new, old).astype(BF16)
         return 0
 
-    def attend(i, k):
-        base = i * GROUP
-        lses = lse_ref[pl.ds(k * H, H), :]
+    def score(i, s_out):
         for u in range(0, GROUP, 2):
-            b = base + u
+            b = i * GROUP + u
             q0 = q3[pl.ds(pl.multiple_of(b * H, H), H), :].astype(BF16)
             q1 = q3[pl.ds(pl.multiple_of(b * H + H, H), H), :].astype(BF16)
             lhs = jnp.concatenate([jnp.concatenate([q0, zero], 1), jnp.concatenate([zero, q1], 1)], 0)
             keys = jnp.concatenate([kbuf[b], kbuf[b + 1]], 1)
+            s_out[u * H:(u + 2) * H, :] = lax.dot_general(lhs, keys, (((1,), (1,)), ((), ())), preferred_element_type=F32)
+
+    def soften(i, s_in, p_out, k):
+        lses = lse_ref[pl.ds(k * H, H), :]
+        for u in range(GROUP):
+            b = i * GROUP + u
+            se = jnp.where(pos <= lens[b] - first, s_in[u * H:(u + 1) * H, :] * QSCALE, NEG)
+            m = jnp.max(se, axis=1, keepdims=True)
+            p = jnp.exp2(se - m)
+            l = jnp.sum(p, axis=1, keepdims=True)
+            p_out[u * H:(u + 1) * H, :] = (p * (1.0 / l)).astype(BF16)
+            lses = jnp.where(lane == b - k * CS, m + jnp.log2(l), lses)
+        lse_ref[pl.ds(k * H, H), :] = lses
+
+    def weigh(i, p_in):
+        for u in range(0, GROUP, 2):
+            b = i * GROUP + u
             vals = jnp.concatenate([vbuf[b], vbuf[b + 1]], 1)
-            s = lax.dot_general(lhs, keys, (((1,), (1,)), ((), ())), preferred_element_type=F32)
-            ps, ls, ms = [], [], []
+            o = jnp.dot(p_in[u * H:(u + 2) * H, :], vals, preferred_element_type=F32)
             for e in range(2):
-                se = jnp.where(pos <= lens[b + e] - first, s[e * H:(e + 1) * H] * QSCALE, NEG)
-                m = jnp.max(se, axis=1, keepdims=True)
-                p = jnp.exp2(se - m)
-                ps.append(p)
-                ms.append(m)
-                ls.append(jnp.sum(p, axis=1, keepdims=True))
-            o = jnp.dot(jnp.concatenate(ps, 0).astype(BF16), vals, preferred_element_type=F32)
-            for e in range(2):
-                o_ref[pl.ds(pl.multiple_of((b + e) * H, H), H), :] = o[e * H:(e + 1) * H, e * DH:(e + 1) * DH] / ls[e]
-                lses = jnp.where(lane == b + e - k * CS, ms[e] + jnp.log2(ls[e]), lses)
-        lse_ref[pl.ds(k * H, H), :] = lses
-        return k
+                o_ref[pl.ds(pl.multiple_of((b + e) * H, H), H), :] = o[e * H:(e + 1) * H, e * DH:(e + 1) * DH]
+
+    def attend(k):
+        lo, hi = k * CS // GROUP, (k + 1) * CS // GROUP
+        score(lo, s_a)
+        score(lo + 1, s_b)
+        soften(lo, s_a, p_a, k)
+
+        def body(t, _):
+            i = lo + 2 + 2 * t
+            score(i, s_a)
+            soften(i - 1, s_b, p_b, k)
+            weigh(i - 2, p_a)
+            score(i + 1, s_b)
+            soften(i, s_a, p_a, k)
+            weigh(i - 1, p_b)
+            return 0
+
+        lax.fori_loop(0, (hi - lo - 2) // 2, body, 0)
+        soften(hi - 1, s_b, p_b, k)
+        weigh(hi - 2, p_a)
+        weigh(hi - 1, p_b)
 
     stores = []
     for k in range(NC):
@@ -121,7 +145,7 @@
         load_v[k].wait()
         lse_ref[pl.ds(k * H, H), :] = jnp.zeros((H, DH), F32)
         lax.fori_loop(k * CS, (k + 1) * CS, insert, 0, unroll=4)
-        lax.fori_loop(k * CS // GROUP, (k + 1) * CS // GROUP, lambda i, c, k=k: attend(i, k), k)
+        attend(k)
         rows = pl.ds(k * CS, CS)
         for e, (buf, out) in enumerate(((kbuf, ko_hbm), (vbuf, vo_hbm))):
             st = pltpu.make_async_copy(buf.at[rows], out.at[rows], osem.at[2 * k + e])
@@ -235,15 +259,9 @@
         rows = rows_of(k, 1 - x, 1 - tp)
         hopd[k].append(send(y_ref.at[rows], y_ref.at[rows], ds.at[k, 3], dr.at[k, 3], mate))
 
-    for step in range(NC + 3):
-        if step < NC:
-            project(step)
-        if 0 <= step - 1 < NC:
-            finish(step - 1)
-        if 0 <= step - 2 < NC:
-            relay(step - 2)
-        if 0 <= step - 3 < NC:
-            last(step - 3)
+    for step, k in ((project, 0), (project, 1), (finish, 0), (project, 2), (finish, 1), (project, 3), (relay, 0), (finish, 2),
+                    (relay, 1), (last, 0), (finish, 3), (relay, 2), (last, 1), (relay, 3), (last, 2), (last, 3)):
+        step(k)
     for k in range(NC):
         for cp in hopd[k]:
             cp.wait_recv()
@@ -266,6 +284,8 @@
                 pltpu.VMEM((B, D), BF16), pltpu.VMEM((B, D), BF16), pltpu.VMEM((D, H * DH), BF16), pltpu.VMEM((D, 2 * DH), BF16),
                 pltpu.VMEM((B * H, DH), F32), pltpu.VMEM((2 * B, DH), F32),
                 pltpu.VMEM((B, T, DH), BF16), pltpu.VMEM((B, T, DH), BF16),
+                pltpu.VMEM((GROUP * H, T), F32), pltpu.VMEM((GROUP * H, T), F32),
+                pltpu.VMEM((GROUP * H, T), BF16), pltpu.VMEM((GROUP * H, T), BF16),
                 pltpu.SemaphoreType.DMA((NQ + 2,)), pltpu.SemaphoreType.DMA((NC,)), pltpu.SemaphoreType.DMA((NC,)),
                 pltpu.SemaphoreType.DMA((2 * NC,)),
             ],

time: 109 us -> 81.7 us (0.75)
  Pallas kernels: 106 us -> 78.9 us
    pallas_call x1, Pallas kernels: 60.3 us -> 32.7 us  [local_step(): pl.pallas_call(attention_kernel, out_shape=(pltpu.VMEM((B * H, DH), F32),...]
where the time goes in v2:
time: 81.7 us; the launch traced here: 81.5 us
  Pallas kernels  78.9 us (97%)
  other arithmetic  1.93 us (2%)
    pallas_call x1, Pallas kernels, local_step(): pl.pallas_call(combine_kernel, out_shape=pltpu.VMEM((B, D), F32), in_spec...  46.2 us
    pallas_call x1, Pallas kernels, local_step(): pl.pallas_call(attention_kernel, out_shape=(pltpu.VMEM((B * H, DH), F32),...  32.7 us
    convert_element_type x1, other arithmetic, local_step(): out_hidden = (hidden.astype(F32) + y + b_out).astype(BF16)  1.93 us

profile of v2, /device:TPU:0, one launch (start us, length us, event | category | flops | bytes accessed | tf_op | source)
XLA Modules:
  0.0 81.5 jit_solution(8311345758488456997)
XLA Ops:
  0.6 32.7 %attention.1 = (f32[4096,128]{1,0:T(8,128)S(1)}, f32[64,128]{1,0:T(8,128)S(1)}, bf16[256,256,128]{2,1,0:T(8,128)(2,1)}, bf16[256,256,128]{2,1,0:T(8,128)(2,1)}) custom-call(s32[256]{0:T(256)} %lens.1, bf16[256,4096]{1,0:T(8,128)(2,1)} %hid_hbm.1, bf16[256,256,128]{2,1,0:T(8,128)(2,1)} %k_hbm.1, bf16[256,256,128]{2,1,0:T(8,128)(2,1)} %v_hbm.1, ...), custom_call_target="tpu_custom_call" | custom-call | tf_op jit(solution)/shard_map/attention/pallas_call | solution.py:278
  33.4 0.0 copy-start
  33.4 0.0 copy-start.1
  33.4 46.2 %combine.1 = f32[256,4096]{1,0:T(8,128)S(1)} custom-call(f32[4096,128]{1,0:T(8,128)S(1)} %get-tuple-element.7.o_ref, f32[64,128]{1,0:T(8,128)S(1)} %get-tuple-element.8.lse_ref, bf16[2048,4096]{1,0:T(8,128)(2,1)} %wo_hbm.1), custom_call_target="tpu_custom_call" | custom-call | tf_op jit(solution)/shard_map/combine/pallas_call | solution.py:296
  79.6 0.0 copy-done
  79.6 0.0 copy-done.1
  79.6 1.9 %add_convert_fusion = bf16[256,4096]{1,0:T(8,128)(2,1)} fusion(f32[256,4096]{1,0:T(8,128)S(1)} %combine.1, bf16[256,4096]{1,0:T(8,128)(2,1)S(1)} %copy-done, f32[4096]{0:T(1024)S(1)} %copy-done.1), kind=kLoop, calls=%fused_computation | loop fusion | flops 4194304 | bytes 8404992 | tf_op jit(solution)/shard_map/convert_element_type | solution.py:314
Async XLA Ops:
  33.4 46.2 %copy-start = (bf16[256,4096]{1,0:T(8,128)(2,1)S(1)}, bf16[256,4096]{1,0:T(8,128)(2,1)}, u32[]{:S(2)}) copy-start(bf16[256,4096]{1,0:T(8,128)(2,1)} %hid_hbm.1) | copy-start | bytes 6291460
  33.4 46.2 %copy-start.1 = (f32[4096]{0:T(1024)S(1)}, f32[4096]{0:T(1024)}, u32[]{:S(2)}) copy-start(f32[4096]{0:T(1024)} %param.23) | copy-start | bytes 49156

commit v3 on v1

v3 whole, which is shorter than its diff:
```python
import functools
import math

import jax
import jax.numpy as jnp
from jax import lax
from jax.experimental import pallas as pl
from jax.experimental.pallas import tpu as pltpu
from jax.sharding import PartitionSpec as P

MESH = pl.DeviceIdType.MESH
F32 = jnp.float32
BF16 = jnp.bfloat16
NEG = -1e30
B = 256
D = 4096
H = 16
DH = 128
T = 256
NC = 4
CS = B // NC
S = CS // 4
HALF = S // 2
QB = 512
NQ = H * DH // QB
QSCALE = DH ** -0.5 * math.log2(math.e)
GROUP = 8
MIB = 1024 * 1024
MLIM = 27
VIA_Y = 768
SCHEDULE = [(s[0], int(s[1])) for s in "a1 s1 a2 m1 s2 p0 m2 a3 s3 p1 m3 f0 p2 f1 r0 p3 f2 r1 l0 f3 r2 l1 r3 l2 l3".split()]


def attention_stages(lens, first, q3, kbuf, vbuf, base, vbase, kv, o_ref, lse_ref, bufs):
    lane = lax.broadcasted_iota(jnp.int32, (H, DH), 1)
    pos = lax.broadcasted_iota(jnp.int32, (H, T), 1)
    zero = jnp.zeros((H, DH), BF16)
    s_a, s_b, p_a, p_b, r_a, r_b, n_a, n_b = bufs

    def score(i, s_out):
        for u in range(0, GROUP, 2):
            b = i * GROUP + u
            q0 = q3[pl.ds(pl.multiple_of(b * H, H), H), :].astype(BF16)
            q1 = q3[pl.ds(pl.multiple_of(b * H + H, H), H), :].astype(BF16)
            lhs = jnp.concatenate([jnp.concatenate([q0, zero], 1), jnp.concatenate([zero, q1], 1)], 0)
            keys = jnp.concatenate([kbuf[b - base], kbuf[b + 1 - base]], 1)
            s_out[u * H:(u + 2) * H, :] = lax.dot_general(lhs, keys, (((1,), (1,)), ((), ())), preferred_element_type=F32)

    def soften(i, s_in, p_out, r_out, n_out, k):
        lses = lse_ref[pl.ds(k * H, H), :]
        for u in range(GROUP):
            b = i * GROUP + u
            row = lens[b] - first
            here = jnp.logical_and(row >= 0, row < T)
            k_new = kv[pl.ds(b, 1), :]
            v_new = kv[pl.ds(B + b, 1), :]
            q_row = q3[pl.ds(pl.multiple_of(b * H, H), H), :]
            s_new = jnp.where(here, jnp.sum(q_row * k_new, axis=1, keepdims=True) * QSCALE, NEG)
            se = jnp.where(pos < row, s_in[u * H:(u + 1) * H, :] * QSCALE, NEG)
            m = jnp.maximum(jnp.max(se, axis=1, keepdims=True), s_new)
            p = jnp.exp2(se - m)
            p_new = jnp.exp2(s_new - m)
            l = jnp.sum(p, axis=1, keepdims=True) + p_new
            r = 1.0 / l
            p_out[u * H:(u + 1) * H, :] = p.astype(BF16)
            r_out[u * H:(u + 1) * H, :] = jnp.broadcast_to(r, (H, DH))
            n_out[u * H:(u + 1) * H, :] = (p_new * r) * v_new
            lses = jnp.where(lane == b - k * CS, m + jnp.log2(l), lses)
        lse_ref[pl.ds(k * H, H), :] = lses

    def weigh(i, p_in, r_in, n_in):
        for u in range(0, GROUP, 2):
            b = i * GROUP + u
            vals = jnp.concatenate([vbuf[b - vbase], vbuf[b + 1 - vbase]], 1)
            o = jnp.dot(p_in[u * H:(u + 2) * H, :], vals, preferred_element_type=F32)
            for e in range(2):
                part = slice((u + e) * H, (u + e + 1) * H)
                o_ref[pl.ds(pl.multiple_of((b + e) * H, H), H), :] = (
                    o[e * H:(e + 1) * H, e * DH:(e + 1) * DH] * r_in[part, :] + n_in[part, :])

    def attend(k):
        lse_ref[pl.ds(k * H, H), :] = jnp.zeros((H, DH), F32)
        lo, hi = k * CS // GROUP, (k + 1) * CS // GROUP
        score(lo, s_a)
        score(lo + 1, s_b)
        soften(lo, s_a, p_a, r_a, n_a, k)

        def body(t, _):
            i = lo + 2 + 2 * t
            score(i, s_a)
            soften(i - 1, s_b, p_b, r_b, n_b, k)
            weigh(i - 2, p_a, r_a, n_a)
            score(i + 1, s_b)
            soften(i, s_a, p_a, r_a, n_a, k)
            weigh(i - 1, p_b, r_b, n_b)
            return 0

        lax.fori_loop(0, (hi - lo - 2) // 2, body, 0)
        soften(hi - 1, s_b, p_b, r_b, n_b, k)
        weigh(hi - 2, p_a, r_a, n_a)
        weigh(hi - 1, p_b, r_b, n_b)

    return attend


STAGE_BUFS = [pltpu.VMEM((GROUP * H, T), F32)] * 2 + [pltpu.VMEM((GROUP * H, T), BF16)] * 2 + [pltpu.VMEM((GROUP * H, DH), F32)] * 4


def insert_rows(lens, first, kv, pairs, lo, hi, base):
    sub = lax.broadcasted_iota(jnp.int32, (16, DH), 0)

    def insert(b, _):
        row = lens[b] - first
        start = pl.multiple_of((jnp.clip(row, 0, T - 1) // 16) * 16, 16)
        hit = sub == row - start
        for c, buf in enumerate(pairs):
            new = kv[pl.ds(c * B + b, 1), :]
            old = buf[b - base, pl.ds(start, 16), :].astype(F32)
            buf[b - base, pl.ds(start, 16), :] = jnp.where(hit, new, old).astype(BF16)
        return 0

    lax.fori_loop(lo, hi, insert, 0, unroll=4)


def first_kernel(lens, hid_hbm, k_hbm, v_hbm, gain_ref, bias_ref, wq_hbm, bq_ref, wkv_hbm, bkv_ref,
                 q3, kv, o_ref, lse_ref, ko_hbm, vo_hbm,
                 hid, h, wq, wkv, kbuf, vbuf, b0, b1, b2, b3, b4, b5, b6, b7, wsem, csem):
    first = lax.axis_index("sq") * T
    load_h = pltpu.make_async_copy(hid_hbm, hid, wsem.at[NQ])
    load_h.start()
    load_wkv = pltpu.make_async_copy(wkv_hbm, wkv, wsem.at[NQ + 1])
    load_wkv.start()
    load_wq = []
    for j in range(NQ):
        cols = pl.ds(j * QB, QB)
        load_wq.append(pltpu.make_async_copy(wq_hbm.at[:, cols], wq.at[:, cols], wsem.at[j]))
        load_wq[-1].start()
    loads = [pltpu.make_async_copy(src.at[pl.ds(0, CS)], dst, csem.at[e]) for e, (src, dst) in enumerate(((k_hbm, kbuf), (v_hbm, vbuf)))]
    for c in loads:
        c.start()
    load_h.wait()

    def norm_rows(i, _):
        rows = pl.ds(pl.multiple_of(i * 16, 16), 16)
        x = hid[rows, :].astype(F32)
        mean = jnp.sum(x, axis=-1, keepdims=True) * (1.0 / D)
        cen = x - mean
        var = jnp.sum(cen * cen, axis=-1, keepdims=True) * (1.0 / D)
        y = cen * lax.rsqrt(var + 1e-5)
        h[rows, :] = (y * gain_ref[...] + bias_ref[...]).astype(BF16)
        return 0

    lax.fori_loop(0, B // 16, norm_rows, 0, unroll=2)
    load_wkv.wait()
    new_kv = (jnp.dot(h[...], wkv[...], preferred_element_type=F32) + bkv_ref[...]).astype(BF16).astype(F32)
    kv[0:B, :] = new_kv[:, :DH]
    kv[B:2 * B, :] = new_kv[:, DH:]
    for j in range(NQ):
        load_wq[j].wait()
        cols = pl.ds(j * QB, QB)
        q = jnp.dot(h[...], wq[:, cols], preferred_element_type=F32) + bq_ref[:, cols]
        q = q.astype(BF16).astype(F32)
        for n in range(QB // DH):
            q3[pl.ds(j * (QB // DH) + n, B, stride=H), :] = q[:, n * DH:(n + 1) * DH]
    for c in loads:
        c.wait()
    insert_rows(lens, first, kv, (kbuf, vbuf), 0, CS, 0)
    stores = [pltpu.make_async_copy(src, dst.at[pl.ds(0, CS)], csem.at[2 + e]) for e, (src, dst) in enumerate(((kbuf, ko_hbm), (vbuf, vo_hbm)))]
    for c in stores:
        c.start()
    attention_stages(lens, first, q3, kbuf, vbuf, 0, 0, kv, o_ref, lse_ref, (b0, b1, b2, b3, b4, b5, b6, b7))(0)
    for c in stores:
        c.wait()


def column(tile, j):
    return tile[:, j:j + 1]


def merge(la, lb):
    top = jnp.maximum(la, lb)
    wa, wb = jnp.exp2(la - top), jnp.exp2(lb - top)
    tot = wa + wb
    return wa / tot, wb / tot, top + jnp.log2(tot)


def exchange_kernel(lens, q3, kv, o_first, lse_first, k_hbm, v_hbm, wo_hbm, y_ref, held,
                    wo, o_ref, lse_ref, b0, b1, b2, b3, b4, b5, b6, b7, o_core, l_core, o_mix, l_mix, o_x, l_x, a3, part, p_y,
                    wsem, csem, a0s, a0r, a1s, a1r, bs, br, cs, cr, ds, dr):
    sq, tp = lax.axis_index("sq"), lax.axis_index("tp")
    x, c = sq // 2, sq % 2
    mate = {"sq": x * 2 + 1 - c}
    over_x = {"sq": (1 - x) * 2 + c}
    over_y = {"tp": 1 - tp}
    loads = {}

    def fetch(k):
        rows = pl.ds(k * CS, CS)
        loads[k] = [pltpu.make_async_copy(src.at[rows], held.at[pl.ds((k - 1) * CS + e * (B - CS), CS)], csem.at[2 * k + e - 2])
                    for e, src in enumerate((k_hbm, v_hbm))]
        for cp in loads[k]:
            cp.start()

    fetch(1)
    fetch(2)
    load = pltpu.make_async_copy(wo_hbm, wo, wsem)
    load.start()
    fetch(3)
    bar = pltpu.get_barrier_semaphore()
    for dev in (mate, over_x, over_y):
        pl.semaphore_signal(bar, inc=1, device_id=dev, device_id_type=MESH)
    pl.semaphore_wait(bar, 3)

    def send(src, dst, ssem, rsem, dev):
        cp = pltpu.make_async_remote_copy(src, dst, ssem, rsem, device_id=dev, device_id_type=MESH)
        cp.start()
        return cp

    W = 2 * S * H
    hop0, hop1, hopb, hopc, hopd = {}, {}, {}, {}, {}
    stages = attention_stages(lens, sq * T, q3, held, held, CS, CS - (B - CS), kv, o_ref, lse_ref, (b0, b1, b2, b3, b4, b5, b6, b7))

    def attend(k):
        for cp in loads[k]:
            cp.wait()
        stages(k)

    def source(k):
        return (o_first, lse_first) if k == 0 else (o_ref, lse_ref)

    def share(k):
        o_k, l_k = source(k)
        other = pl.multiple_of(k * CS * H + (1 - c) * W, W)
        hop0[k] = (send(o_k.at[pl.ds(other, W)], o_core.at[k], a0s.at[k, 0], a0r.at[k, 0], mate),
                   send(l_k.at[pl.ds(k * H, H)], l_core.at[k], a0s.at[k, 1], a0r.at[k, 1], mate))

    def mix(k):
        o_k, l_k = source(k)
        for cp in hop0[k]:
            cp.wait_recv()
        shift = lax.rem(DH - c * 2 * S, DH)
        fa, fb, lm = merge(pltpu.roll(l_k[pl.ds(k * H, H), :], shift, 1), pltpu.roll(l_core[k], shift, 1))
        l_mix[k] = lm
        mine = k * CS * H + c * W
        for j in range(2 * S):
            oa = o_k[pl.ds(pl.multiple_of(mine + j * H, H), H), :]
            ob = o_core[k, j * H:(j + 1) * H, :]
            o_mix[k, j * H:(j + 1) * H, :] = column(fa, j) * oa + column(fb, j) * ob
        far = pl.multiple_of((1 - x) * S * H, S * H)
        hop1[k] = (send(o_mix.at[k, pl.ds(far, S * H)], o_x.at[k], a1s.at[k, 0], a1r.at[k, 0], over_x),
                   send(l_mix.at[k], l_x.at[k], a1s.at[k, 1], a1r.at[k, 1], over_x))

    def project(k):
        for cp in hop1[k]:
            cp.wait_recv()
        shift = lax.rem(DH - x * S, DH)
        fa, fb, _ = merge(pltpu.roll(l_mix[k], shift, 1), pltpu.roll(l_x[k], shift, 1))
        near = x * S * H
        for j in range(S):
            oa = o_mix[k, pl.ds(pl.multiple_of(near + j * H, H), H), :]
            ob = o_x[k, j * H:(j + 1) * H, :]
            a3[j * H:(j + 1) * H, :] = column(fa, j) * oa + column(fb, j) * ob
        a = jnp.concatenate([a3[pl.ds(n, S, stride=H), :].astype(BF16) for n in range(H)], 1)
        if k == 0:
            load.wait()

        def cols(i, _):
            cc = pl.ds(pl.multiple_of(i * 1024, 1024), 1024)
            part[k, :, cc] = jnp.dot(a, wo[:, cc], preferred_element_type=F32)
            return 0

        lax.fori_loop(0, D // 1024, cols, 0)
        far = pl.multiple_of((1 - tp) * HALF, HALF)
        hopb[k] = send(part.at[k, pl.ds(far, HALF)], p_y.at[k], bs.at[k], br.at[k], over_y)

    def rows_of(k, xx, yy):
        return pl.ds(pl.multiple_of(k * CS + (c * 2 + xx) * S + yy * HALF, HALF), HALF)

    def finish(k):
        hopb[k].wait_recv()
        rows = rows_of(k, x, tp)
        y_ref[rows, :] = part[k, pl.ds(pl.multiple_of(tp * HALF, HALF), HALF), :] + p_y[k]
        hopc[k] = [send(y_ref.at[rows], y_ref.at[rows], cs.at[k, 0], cr.at[k, 0], over_x),
                   send(y_ref.at[rows], y_ref.at[rows], cs.at[k, 1], cr.at[k, 1], over_y)]
        hopd[k] = [send(y_ref.at[rows], y_ref.at[rows], ds.at[k, 0], dr.at[k, 0], mate)]

    lo, hi = pl.ds(0, VIA_Y), pl.ds(VIA_Y, D - VIA_Y)

    def relay(k):
        hopc[k][1].wait_recv()
        rows = rows_of(k, x, 1 - tp)
        d2 = send(y_ref.at[rows, hi], y_ref.at[rows, hi], cs.at[k, 3], cr.at[k, 3], over_x)
        hopd[k].append(send(y_ref.at[rows], y_ref.at[rows], ds.at[k, 2], dr.at[k, 2], mate))
        hopc[k][0].wait_recv()
        rows = rows_of(k, 1 - x, tp)
        d1 = send(y_ref.at[rows, lo], y_ref.at[rows, lo], cs.at[k, 2], cr.at[k, 2], over_y)
        hopd[k].append(send(y_ref.at[rows], y_ref.at[rows], ds.at[k, 1], dr.at[k, 1], mate))
        hopc[k] += [d1, d2]

    def last(k):
        hopc[k][2].wait_recv()
        hopc[k][3].wait_recv()
        rows = rows_of(k, 1 - x, 1 - tp)
        hopd[k].append(send(y_ref.at[rows], y_ref.at[rows], ds.at[k, 3], dr.at[k, 3], mate))

    share(0)
    mix(0)
    for step, k in SCHEDULE:
        {"a": attend, "s": share, "m": mix, "p": project, "f": finish, "r": relay, "l": last}[step](k)
    for k in range(NC):
        for cp in hopd[k]:
            cp.wait_recv()
    for k in range(NC):
        for cp in [*hop0[k], *hop1[k], hopb[k], *hopc[k], *hopd[k]]:
            cp.wait_send()


def last_kernel(lens, kv, y_in, hid, bo_ref, held, k_part, v_part, ko_hbm, vo_hbm, out_hbm, ktile, vtile, out, sem, tsem):
    first = lax.axis_index("sq") * T
    sub = lax.broadcasted_iota(jnp.int32, (16, DH), 0)
    sides = ((0, ktile, ko_hbm), (B - CS, vtile, vo_hbm))
    copies = []
    for k in range(1, NC):
        for e, (src, _, dst) in enumerate(sides):
            copies.append(pltpu.make_async_copy(held.at[pl.ds(src + (k - 1) * CS, CS)], dst.at[pl.ds(k * CS, CS)], sem.at[2 * k + e - 2]))
            copies[-1].start()

    def rows(i, _):
        r = pl.ds(pl.multiple_of(i * 16, 16), 16)
        out[r, :] = (hid[r, :].astype(F32) + y_in[r, :] + bo_ref[...]).astype(BF16)
        return 0

    lax.fori_loop(0, B // 16, rows, 0, unroll=2)
    store_out = pltpu.make_async_copy(out, out_hbm, sem.at[2 * NC - 2])
    store_out.start()

    def spot(b):
        row = lens[b] - first
        start = pl.multiple_of((jnp.clip(row, 0, T - 1) // 16) * 16, 16)
        return row, start, jnp.logical_and(row >= 0, row < T)

    def build(b, _):
        row, start, _ = spot(b)
        hit = sub == row - start
        for c, (src, tile, _) in enumerate(sides):
            new = kv[pl.ds(c * B + b, 1), :]
            old = held[b - CS + src, pl.ds(start, 16), :].astype(F32)
            tile[b - CS] = jnp.where(hit, new, old).astype(BF16)
        return 0

    lax.fori_loop(CS, B, build, 0, unroll=4)

    def tile_copy(b, start, side):
        return pltpu.make_async_copy(side[1].at[b - CS], side[2].at[b, pl.ds(start, 16), :], tsem)

    def put(b, _):
        _, start, own = spot(b)

        @pl.when(own)
        def _():
            for side in sides:
                tile_copy(b, start, side).start()
        return 0

    def drain(b, _):
        _, start, own = spot(b)

        @pl.when(own)
        def _():
            for side in sides:
                tile_copy(b, start, side).wait()
        return 0

    for k in range(1, NC):
        copies[2 * k - 2].wait()
        copies[2 * k - 1].wait()
        lax.fori_loop(k * CS, (k + 1) * CS, put, 0)
    store_out.wait()
    lax.fori_loop(CS, B, drain, 0)


def solution(mesh):
    def local_step(hidden, cache_lens, k_cache, v_cache, ln_gain, ln_bias, w_query, b_query, w_kv, b_kv, w_out, b_out):
        hbm = pl.BlockSpec(memory_space=pltpu.HBM)
        vm = pl.BlockSpec(memory_space=pltpu.VMEM)
        smem = pl.BlockSpec(memory_space=pltpu.SMEM)
        sem = pltpu.SemaphoreType.DMA

        def pin(*arrays):
            return [pltpu.with_memory_space_constraint(a, pltpu.VMEM) for a in arrays]

        def far(*arrays):
            return [pltpu.with_memory_space_constraint(a, pltpu.HBM) for a in arrays]

        cache = jax.ShapeDtypeStruct((B, T, DH), BF16)
        q3, kv, o0, lse0, k_part, v_part = pl.pallas_call(
            first_kernel,
            out_shape=(pltpu.VMEM((B * H, DH), F32), pltpu.VMEM((2 * B, DH), F32), pltpu.VMEM((CS * H, DH), F32), pltpu.VMEM((H, DH), F32), cache, cache),
            in_specs=[smem, hbm, hbm, hbm, vm, vm, hbm, vm, hbm, vm],
            out_specs=(vm, vm, vm, vm, hbm, hbm),
            scratch_shapes=[
                pltpu.VMEM((B, D), BF16), pltpu.VMEM((B, D), BF16), pltpu.VMEM((D, H * DH), BF16), pltpu.VMEM((D, 2 * DH), BF16),
                pltpu.VMEM((CS, T, DH), BF16), pltpu.VMEM((CS, T, DH), BF16), *STAGE_BUFS, sem((NQ + 2,)), sem((4,)),
            ],
            compiler_params=pltpu.CompilerParams(vmem_limit_bytes=33 * MIB),
            name="first",
        )(*far(cache_lens, hidden, k_cache, v_cache, ln_gain[None], ln_bias[None], w_query, b_query[None], w_kv, b_kv[None]))
        held = pltpu.VMEM((2 * (B - CS), T, DH), BF16)
        y, kv_held = pl.pallas_call(
            exchange_kernel,
            out_shape=(pltpu.VMEM((B, D), F32), held),
            in_specs=[smem, vm, vm, vm, vm, hbm, hbm, hbm],
            out_specs=(vm, vm),
            scratch_shapes=[
                pltpu.VMEM((H * DH, D), BF16), pltpu.VMEM((B * H, DH), F32), pltpu.VMEM((NC * H, DH), F32), *STAGE_BUFS,
                pltpu.VMEM((NC, 2 * S * H, DH), F32), pltpu.VMEM((NC, H, DH), F32),
                pltpu.VMEM((NC, 2 * S * H, DH), F32), pltpu.VMEM((NC, H, DH), F32),
                pltpu.VMEM((NC, S * H, DH), F32), pltpu.VMEM((NC, H, DH), F32),
                pltpu.VMEM((S * H, DH), F32),
                pltpu.VMEM((NC, S, D), F32), pltpu.VMEM((NC, HALF, D), F32),
                sem, sem((2 * NC - 2,)), sem((NC, 2)), sem((NC, 2)), sem((NC, 2)), sem((NC, 2)), sem((NC,)), sem((NC,)),
                sem((NC, 4)), sem((NC, 4)), sem((NC, 4)), sem((NC, 4)),
            ],
            compiler_params=pltpu.CompilerParams(vmem_limit_bytes=MLIM * MIB, collective_id=0, has_side_effects=True),
            name="exchange",
        )(*far(cache_lens), *pin(q3, kv, o0, lse0), *far(k_cache, v_cache, w_out))
        k_new, v_new, out_hidden = pl.pallas_call(
            last_kernel,
            out_shape=(cache, cache, jax.ShapeDtypeStruct((B, D), BF16)),
            in_specs=[smem, vm, vm, vm, vm, vm, hbm, hbm],
            out_specs=(hbm, hbm, hbm),
            input_output_aliases={6: 0, 7: 1},
            scratch_shapes=[pltpu.VMEM((B - CS, 16, DH), BF16), pltpu.VMEM((B - CS, 16, DH), BF16), pltpu.VMEM((B, D), BF16), sem((2 * NC - 1,)), sem],
            compiler_params=pltpu.CompilerParams(vmem_limit_bytes=6 * MIB),
            name="last",
        )(*far(cache_lens), *pin(kv, y), hidden, b_out[None], *pin(kv_held), k_part, v_part)
        return out_hidden, k_new, v_new

    cache_spec = P("dp", "sq", None)
    row_spec = P("dp", None)
    in_specs = (row_spec, P("dp"), cache_spec, cache_spec, P(None), P(None), P(None, "tp"), P("tp"), P(None, None), P(None), P("tp", None), P(None))
    out_specs = (row_spec, cache_spec, cache_spec)
    return jax.shard_map(local_step, mesh=mesh, in_specs=in_specs, out_specs=out_specs, check_vma=False)
```

time: 109 us -> 78.4 us (0.72)
  Pallas kernels: 106 us -> 77.4 us
  other arithmetic: 1.93 us -> 0 us
    pallas_call x2 -> x3, Pallas kernels: 106 us -> 77.4 us  [the longest x1 52.3 us: local_step(): pl.pallas_call(exchange_kernel, out_shape=(pltpu.VMEM((B, D), F32), held)...]
    convert_element_type x1 -> x0, other arithmetic: 1.93 us -> none  [local_step(): out_hidden = (hidden.astype(F32) + y + b_out).astype(BF16)]
where the time goes in v3:
time: 78.4 us; the launch traced here: 78.1 us
  Pallas kernels  77.4 us (99%)
    pallas_call x1, Pallas kernels, local_step(): pl.pallas_call(exchange_kernel, out_shape=(pltpu.VMEM((B, D), F32), held)...  52.3 us
    pallas_call x1, Pallas kernels, local_step(): pl.pallas_call(first_kernel, out_shape=(pltpu.VMEM((B * H, DH), F32), plt...  15.4 us
    pallas_call x1, Pallas kernels, local_step(): pl.pallas_call(last_kernel, out_shape=(cache, cache, jax.ShapeDtypeStruct...  9.77 us

profile of v3, /device:TPU:0, one launch (start us, length us, event | category | flops | bytes accessed | tf_op | source)
XLA Modules:
  0.0 78.1 jit_solution(16641331004736110444)
XLA Ops:
  0.6 15.4 %first.1 = (f32[4096,128]{1,0:T(8,128)S(1)}, f32[512,128]{1,0:T(8,128)S(1)}, f32[1024,128]{1,0:T(8,128)S(1)}, f32[16,128]{1,0:T(8,128)S(1)}, bf16[256,256,128]{2...) custom-call(s32[256]{0:T(256)} %lens.5, bf16[256,4096]{1,0:T(8,128)(2,1)} %hid.1, bf16[256,256,128]{2,1,0:T(8,128)(2,1)} %k_hbm.3, ...), custom_call_target="tpu_custom_call" | custom-call | tf_op jit(solution)/shard_map/first/pallas_call | solution.py:396
  16.1 0.0 copy-start
  16.1 0.0 copy-start.1
  16.1 52.3 %exchange.1 = (f32[256,4096]{1,0:T(8,128)S(1)}, bf16[384,256,128]{2,1,0:T(8,128)(2,1)S(1)}) custom-call(s32[256]{0:T(256)} %lens.5, f32[4096,128]{1,0:T(8,128)S(1)} %get-tuple-element.15.q3, f32[512,128]{1,0:T(8,128)S(1)} %get-tuple-element.14.kv, f32[1024,128]{1,0:T(8,128)S(1)} %get-tuple-element.16.o_first, f32[16,128]{1,0:T(8,128)S(1)} %get-tuple-element.17.lse_first, ...), custom_call_target="tpu_custom_call" | custom-call | tf_op jit(solution)/shard_map/exchange/pallas_call | solution.py:409
  68.3 0.0 copy-done
  68.4 0.0 copy-done.1
  68.4 9.8 %last.1 = (bf16[256,256,128]{2,1,0:T(8,128)(2,1)}, bf16[256,256,128]{2,1,0:T(8,128)(2,1)}, bf16[256,4096]{1,0:T(8,128)(2,1)}) custom-call(s32[256]{0:T(256)} %lens.5, f32[512,128]{1,0:T(8,128)S(1)} %get-tuple-element.14.kv, f32[256,4096]{1,0:T(8,128)S(1)} %get-tuple-element.18.y_in, ...), custom_call_target="tpu_custom_call", output_to_operand_aliasing={{0}: (6, {}), {1}: (7, {})} | custom-call | tf_op jit(solution)/shard_map/last/pallas_call | solution.py:427
Async XLA Ops:
  16.1 52.3 %copy-start = (bf16[256,4096]{1,0:T(8,128)(2,1)S(1)}, bf16[256,4096]{1,0:T(8,128)(2,1)}, u32[]{:S(2)}) copy-start(bf16[256,4096]{1,0:T(8,128)(2,1)} %hid.1) | copy-start | bytes 6291460
  16.1 52.3 %copy-start.1 = (f32[4096]{0:T(1024)S(1)}, f32[4096]{0:T(1024)}, u32[]{:S(2)}) copy-start(f32[4096]{0:T(1024)} %param.23) | copy-start | bytes 49156

commit v4 on v3

v4 whole, which is shorter than its diff:
```python
import functools
import math

import jax
import jax.numpy as jnp
from jax import lax
from jax.experimental import pallas as pl
from jax.experimental.pallas import tpu as pltpu
from jax.sharding import PartitionSpec as P

MESH = pl.DeviceIdType.MESH
F32 = jnp.float32
BF16 = jnp.bfloat16
NEG = -1e30
B = 256
D = 4096
H = 16
DH = 128
T = 256
AB = 64
NC = 8
CS = B // NC
S = CS // 4
R = 2 * S
DC = D // 2
DY = DC // 2
QB = 512
NQ = H * DH // QB
QSCALE = DH ** -0.5 * math.log2(math.e)
GROUP = 8
MIB = 1024 * 1024
VIA_Y = 128
SCHEDULE = [(s[0], int(s[1])) for s in "s0 s1 m0 a2 m1 s2 s3 a4 s4 s5 m2 m3 q0 m4 q1 m5 p0 p1 q2 a6 f0 q3 s6 s7 q4 f1 p2 m6 m7 p3 r0 p4 f2 q5 q6 q7 f3 r1 p5 f4 r2 p6 l0 l1 r3 p7 f5 r4 f6 f7 l2 r5 l3 l4 r6 r7 l5 l6 l7".split()]
def attention_stages(lens, first, q3, kbuf, vbuf, base, vbase, kv, o_ref, lse_ref, bufs):
    lane = lax.broadcasted_iota(jnp.int32, (H, DH), 1)
    pos = lax.broadcasted_iota(jnp.int32, (H, T), 1)
    zero = jnp.zeros((H, DH), BF16)
    s_a, s_b, p_a, p_b, r_a, r_b, n_a, n_b = bufs

    def score(i, s_out):
        for u in range(0, GROUP, 2):
            b = i * GROUP + u
            q0 = q3[pl.ds(pl.multiple_of(b * H, H), H), :].astype(BF16)
            q1 = q3[pl.ds(pl.multiple_of(b * H + H, H), H), :].astype(BF16)
            lhs = jnp.concatenate([jnp.concatenate([q0, zero], 1), jnp.concatenate([zero, q1], 1)], 0)
            keys = jnp.concatenate([kbuf[b - base], kbuf[b + 1 - base]], 1)
            s_out[u * H:(u + 2) * H, :] = lax.dot_general(lhs, keys, (((1,), (1,)), ((), ())), preferred_element_type=F32)

    def soften(i, s_in, p_out, r_out, n_out):
        chunk = lax.div(i * GROUP, CS)
        tile = pl.ds(pl.multiple_of(chunk * H, H), H)
        at = i * GROUP - chunk * CS
        lses = lse_ref[tile, :]
        for u in range(GROUP):
            b = i * GROUP + u
            row = lens[b] - first
            here = jnp.logical_and(row >= 0, row < T)
            k_new = kv[pl.ds(b, 1), :]
            v_new = kv[pl.ds(B + b, 1), :]
            q_row = q3[pl.ds(pl.multiple_of(b * H, H), H), :]
            s_new = jnp.where(here, jnp.sum(q_row * k_new, axis=1, keepdims=True) * QSCALE, NEG)
            se = jnp.where(pos < row, s_in[u * H:(u + 1) * H, :] * QSCALE, NEG)
            m = jnp.maximum(jnp.max(se, axis=1, keepdims=True), s_new)
            p = jnp.exp2(se - m)
            p_new = jnp.exp2(s_new - m)
            l = jnp.sum(p, axis=1, keepdims=True) + p_new
            r = 1.0 / l
            p_out[u * H:(u + 1) * H, :] = p.astype(BF16)
            r_out[u * H:(u + 1) * H, :] = jnp.broadcast_to(r, (H, DH))
            n_out[u * H:(u + 1) * H, :] = (p_new * r) * v_new
            lses = jnp.where(lane == at + u, m + jnp.log2(l), lses)
        lse_ref[tile, :] = lses

    def weigh(i, p_in, r_in, n_in):
        for u in range(0, GROUP, 2):
            b = i * GROUP + u
            vals = jnp.concatenate([vbuf[b - vbase], vbuf[b + 1 - vbase]], 1)
            o = jnp.dot(p_in[u * H:(u + 2) * H, :], vals, preferred_element_type=F32)
            for e in range(2):
                part = slice((u + e) * H, (u + e + 1) * H)
                o_ref[pl.ds(pl.multiple_of((b + e) * H, H), H), :] = (
                    o[e * H:(e + 1) * H, e * DH:(e + 1) * DH] * r_in[part, :] + n_in[part, :])

    def attend(k):
        tiles = slice(k * AB // CS * H, (k + 1) * AB // CS * H)
        lse_ref[tiles, :] = jnp.zeros((AB // CS * H, DH), F32)
        lo, hi = k * AB // GROUP, (k + 1) * AB // GROUP
        score(lo, s_a)
        score(lo + 1, s_b)
        soften(lo, s_a, p_a, r_a, n_a)

        def body(t, _):
            i = lo + 2 + 2 * t
            score(i, s_a)
            soften(i - 1, s_b, p_b, r_b, n_b)
            weigh(i - 2, p_a, r_a, n_a)
            score(i + 1, s_b)
            soften(i, s_a, p_a, r_a, n_a)
            weigh(i - 1, p_b, r_b, n_b)
            return 0

        lax.fori_loop(0, (hi - lo - 2) // 2, body, 0)
        soften(hi - 1, s_b, p_b, r_b, n_b)
        weigh(hi - 2, p_a, r_a, n_a)
        weigh(hi - 1, p_b, r_b, n_b)

    return attend


STAGE_BUFS = [pltpu.VMEM((GROUP * H, T), F32)] * 2 + [pltpu.VMEM((GROUP * H, T), BF16)] * 2 + [pltpu.VMEM((GROUP * H, DH), F32)] * 4


def insert_rows(lens, first, kv, pairs, lo, hi, base):
    sub = lax.broadcasted_iota(jnp.int32, (16, DH), 0)

    def insert(b, _):
        row = lens[b] - first
        start = pl.multiple_of((jnp.clip(row, 0, T - 1) // 16) * 16, 16)
        hit = sub == row - start
        for c, buf in enumerate(pairs):
            new = kv[pl.ds(c * B + b, 1), :]
            old = buf[b - base, pl.ds(start, 16), :].astype(F32)
            buf[b - base, pl.ds(start, 16), :] = jnp.where(hit, new, old).astype(BF16)
        return 0

    lax.fori_loop(lo, hi, insert, 0, unroll=4)


def first_kernel(lens, hid_hbm, k_hbm, v_hbm, gain_ref, bias_ref, wq_hbm, bq_ref, wkv_hbm, bkv_ref,
                 q3, kv, o_ref, lse_ref, ko_hbm, vo_hbm,
                 hid, h, wq, wkv, kbuf, vbuf, b0, b1, b2, b3, b4, b5, b6, b7, wsem, csem):
    first = lax.axis_index("sq") * T
    load_h = []
    for e in range(2):
        rows = pl.ds(e * (B // 2), B // 2)
        load_h.append(pltpu.make_async_copy(hid_hbm.at[rows], hid.at[rows], wsem.at[NQ + e]))
        load_h[-1].start()
    load_wkv = pltpu.make_async_copy(wkv_hbm, wkv, wsem.at[NQ + 2])
    load_wkv.start()
    load_wq = []
    for j in range(NQ):
        cols = pl.ds(j * QB, QB)
        load_wq.append(pltpu.make_async_copy(wq_hbm.at[:, cols], wq.at[:, cols], wsem.at[j]))
        load_wq[-1].start()
    loads = [pltpu.make_async_copy(src.at[pl.ds(0, AB)], dst, csem.at[e]) for e, (src, dst) in enumerate(((k_hbm, kbuf), (v_hbm, vbuf)))]
    for c in loads:
        c.start()

    def norm_rows(i, _):
        rows = pl.ds(pl.multiple_of(i * 16, 16), 16)
        x = hid[rows, :].astype(F32)
        mean = jnp.sum(x, axis=-1, keepdims=True) * (1.0 / D)
        cen = x - mean
        var = jnp.sum(cen * cen, axis=-1, keepdims=True) * (1.0 / D)
        y = cen * lax.rsqrt(var + 1e-5)
        h[rows, :] = (y * gain_ref[...] + bias_ref[...]).astype(BF16)
        return 0

    for e in range(2):
        load_h[e].wait()
        lax.fori_loop(e * (B // 32), (e + 1) * (B // 32), norm_rows, 0, unroll=2)
    load_wkv.wait()
    new_kv = (jnp.dot(h[...], wkv[...], preferred_element_type=F32) + bkv_ref[...]).astype(BF16).astype(F32)
    kv[0:B, :] = new_kv[:, :DH]
    kv[B:2 * B, :] = new_kv[:, DH:]
    for j in range(NQ):
        load_wq[j].wait()
        cols = pl.ds(j * QB, QB)
        q = jnp.dot(h[...], wq[:, cols], preferred_element_type=F32) + bq_ref[:, cols]
        q = q.astype(BF16).astype(F32)
        for n in range(QB // DH):
            q3[pl.ds(j * (QB // DH) + n, B, stride=H), :] = q[:, n * DH:(n + 1) * DH]
    for c in loads:
        c.wait()
    insert_rows(lens, first, kv, (kbuf, vbuf), 0, AB, 0)
    stores = [pltpu.make_async_copy(src, dst.at[pl.ds(0, AB)], csem.at[2 + e]) for e, (src, dst) in enumerate(((kbuf, ko_hbm), (vbuf, vo_hbm)))]
    for c in stores:
        c.start()
    attention_stages(lens, first, q3, kbuf, vbuf, 0, 0, kv, o_ref, lse_ref, (b0, b1, b2, b3, b4, b5, b6, b7))(0)
    for c in stores:
        c.wait()


def column(tile, j):
    return tile[:, j:j + 1]


def merge(la, lb):
    top = jnp.maximum(la, lb)
    wa, wb = jnp.exp2(la - top), jnp.exp2(lb - top)
    tot = wa + wb
    return wa / tot, wb / tot, top + jnp.log2(tot)


def exchange_kernel(lens, q3, kv, o_first, lse_first, k_hbm, v_hbm, wo_hbm, y_ref, held,
                    wo, o_ref, lse_ref, b0, b1, b2, b3, b4, b5, b6, b7, o_core, l_core, o_mix, l_mix, o_x, l_x, a_all, part, p_y,
                    wsem, csem, a0s, a0r, a1s, a1r, a2s, a2r, bs, br, cs, cr, ds, dr):
    sq, tp = lax.axis_index("sq"), lax.axis_index("tp")
    x, c = sq // 2, sq % 2
    mate = {"sq": x * 2 + 1 - c}
    over_x = {"sq": (1 - x) * 2 + c}
    over_y = {"tp": 1 - tp}
    loads = {}

    def fetch(k):
        rows = pl.ds(k * AB, AB)
        loads[k] = [pltpu.make_async_copy(src.at[rows], held.at[pl.ds((k - 1) * AB + e * (B - AB), AB)], csem.at[2 * k + e - 2])
                    for e, src in enumerate((k_hbm, v_hbm))]
        for cp in loads[k]:
            cp.start()

    fetch(1)
    fetch(2)
    load = pltpu.make_async_copy(wo_hbm.at[:, pl.ds(pl.multiple_of(c * DC, DC), DC)], wo, wsem)
    load.start()
    fetch(3)
    bar = pltpu.get_barrier_semaphore()
    for dev in (mate, over_x, over_y):
        pl.semaphore_signal(bar, inc=1, device_id=dev, device_id_type=MESH)
    pl.semaphore_wait(bar, 3)

    def send(src, dst, ssem, rsem, dev):
        cp = pltpu.make_async_remote_copy(src, dst, ssem, rsem, device_id=dev, device_id_type=MESH)
        cp.start()
        return cp

    W = S * H
    hop0, hop1, hop2, hopb, hopc, hopd = {}, {}, {}, {}, {}, {}
    stages = attention_stages(lens, sq * T, q3, held, held, AB, AB - (B - AB), kv, o_ref, lse_ref, (b0, b1, b2, b3, b4, b5, b6, b7))
    ready = []

    def attend(k):
        block = k * CS // AB
        for cp in loads[block]:
            cp.wait()
        stages(block)

    def source(k):
        return (o_first, lse_first) if k * CS < AB else (o_ref, lse_ref)

    def rows_of_o(k, xx, cc):
        return pl.ds(pl.multiple_of((k * 4 + xx * 2 + cc) * W, W), W)

    def share(k):
        o_k, l_k = source(k)
        hop0[k] = [send(o_k.at[rows_of_o(k, xx, 1 - c)], o_core.at[k, xx], a0s.at[k, xx], a0r.at[k, xx], mate) for xx in range(2)]
        hop0[k].append(send(l_k.at[pl.ds(k * H, H)], l_core.at[k], a0s.at[k, 2], a0r.at[k, 2], mate))

    def mix(k):
        o_k, l_k = source(k)
        for cp in hop0[k]:
            cp.wait_recv()
        shift = lax.rem(DH - c * S, DH)
        fa, fb, lm = merge(pltpu.roll(l_k[pl.ds(k * H, H), :], shift, 1), pltpu.roll(l_core[k], shift, 1))
        l_mix[k] = lm
        for xx in range(2):
            mine = (k * 4 + xx * 2 + c) * W
            for j in range(S):
                oa = o_k[pl.ds(pl.multiple_of(mine + j * H, H), H), :]
                ob = o_core[k, xx, j * H:(j + 1) * H, :]
                at = xx * R + j
                o_mix[k, xx, j * H:(j + 1) * H, :] = column(fa, at) * oa + column(fb, at) * ob
        hop1[k] = [send(o_mix.at[k, 1 - x], o_x.at[k], a1s.at[k, 0], a1r.at[k, 0], over_x),
                   send(l_mix.at[k], l_x.at[k], a1s.at[k, 1], a1r.at[k, 1], over_x)]

    def quarter(k):
        for cp in hop1[k]:
            cp.wait_recv()
        shift = lax.rem(DH - x * R, DH)
        fa, fb, _ = merge(pltpu.roll(l_mix[k], shift, 1), pltpu.roll(l_x[k], shift, 1))
        for j in range(S):
            oa = o_mix[k, x, j * H:(j + 1) * H, :]
            ob = o_x[k, j * H:(j + 1) * H, :]
            a_all[k, pl.ds(pl.multiple_of(c * W + j * H, H), H), :] = column(fa, j) * oa + column(fb, j) * ob
        own = pl.ds(pl.multiple_of(c * W, W), W)
        hop2[k] = send(a_all.at[k, own], a_all.at[k, own], a2s.at[k], a2r.at[k], mate)

    def project(k):
        hop2[k].wait_recv()
        a = jnp.concatenate([a_all[k, pl.ds(n, R, stride=H), :].astype(BF16) for n in range(H)], 1)
        if not ready:
            load.wait()
            ready.append(1)
        part[k] = jnp.dot(a, wo[...], preferred_element_type=F32)
        hopb[k] = send(part.at[k, :, pl.ds(pl.multiple_of((1 - tp) * DY, DY), DY)], p_y.at[k], bs.at[k], br.at[k], over_y)

    def piece(k, xx, yy, lo=0, width=DY):
        return (pl.ds(pl.multiple_of(k * CS + xx * R, R), R), pl.ds(pl.multiple_of(c * DC + yy * DY + lo, 128), width))

    def pass_on(at, ssem, rsem, dev):
        return send(y_ref.at[at], y_ref.at[at], ssem, rsem, dev)

    def finish(k):
        hopb[k].wait_recv()
        at = piece(k, x, tp)
        y_ref[at] = part[k, :, pl.ds(pl.multiple_of(tp * DY, DY), DY)] + p_y[k]
        hopc[k] = [pass_on(at, cs.at[k, 0], cr.at[k, 0], over_x), pass_on(at, cs.at[k, 1], cr.at[k, 1], over_y)]
        hopd[k] = [pass_on(at, ds.at[k, 0], dr.at[k, 0], mate)]

    def relay(k):
        hopc[k][1].wait_recv()
        hopc[k].append(pass_on(piece(k, x, 1 - tp, VIA_Y, DY - VIA_Y), cs.at[k, 2], cr.at[k, 2], over_x))
        hopd[k].append(pass_on(piece(k, x, 1 - tp), ds.at[k, 1], dr.at[k, 1], mate))
        hopc[k][0].wait_recv()
        hopc[k].append(pass_on(piece(k, 1 - x, tp, 0, VIA_Y), cs.at[k, 3], cr.at[k, 3], over_y))
        hopd[k].append(pass_on(piece(k, 1 - x, tp), ds.at[k, 2], dr.at[k, 2], mate))

    def last(k):
        hopc[k][2].wait_recv()
        hopc[k][3].wait_recv()
        hopd[k].append(pass_on(piece(k, 1 - x, 1 - tp), ds.at[k, 3], dr.at[k, 3], mate))

    for step, k in SCHEDULE:
        {"a": attend, "s": share, "m": mix, "q": quarter, "p": project, "f": finish, "r": relay, "l": last}[step](k)
    for k in range(NC):
        for cp in hopd[k]:
            cp.wait_recv()
    for k in range(NC):
        for cp in [*hop0[k], *hop1[k], hop2[k], hopb[k], *hopc[k], *hopd[k]]:
            cp.wait_send()


def last_kernel(lens, kv, y_in, hid, bo_ref, held, k_part, v_part, ko_hbm, vo_hbm, out_hbm, ktile, vtile, out, sem, osem, tsem):
    first = lax.axis_index("sq") * T
    sub = lax.broadcasted_iota(jnp.int32, (16, DH), 0)
    sides = ((0, ktile, ko_hbm), (B - AB, vtile, vo_hbm))
    blocks = range(1, B // AB)
    copies = {}
    for k in blocks:
        for e, (src, _, dst) in enumerate(sides):
            copies[k, e] = pltpu.make_async_copy(held.at[pl.ds(src + (k - 1) * AB, AB)], dst.at[pl.ds(k * AB, AB)], sem.at[2 * k + e - 2])
            copies[k, e].start()

    def rows(i, _):
        r = pl.ds(pl.multiple_of(i * 16, 16), 16)
        out[r, :] = (hid[r, :].astype(F32) + y_in[r, :] + bo_ref[...]).astype(BF16)
        return 0

    lax.fori_loop(0, B // 16, rows, 0, unroll=2)
    store_out = pltpu.make_async_copy(out, out_hbm, osem)
    store_out.start()

    def spot(b):
        row = lens[b] - first
        start = pl.multiple_of((jnp.clip(row, 0, T - 1) // 16) * 16, 16)
        return row, start

    def build(b, _):
        row, start = spot(b)
        hit = sub == row - start
        for c, (src, tile, _) in enumerate(sides):
            new = kv[pl.ds(c * B + b, 1), :]
            old = held[b - AB + src, pl.ds(start, 16), :].astype(F32)
            tile[b - AB] = jnp.where(hit, new, old).astype(BF16)
        return 0

    lax.fori_loop(AB, B, build, 0, unroll=4)

    def put(b, _):
        _, start = spot(b)
        for e, (_, tile, dst) in enumerate(sides):
            pltpu.make_async_copy(tile.at[b - AB], dst.at[b, pl.ds(start, 16), :], tsem.at[e]).start()
        return 0

    for k in blocks:
        for e in range(2):
            copies[k, e].wait()
        lax.fori_loop(k * AB, (k + 1) * AB, put, 0, unroll=4)
    store_out.wait()
    for e, (_, tile, dst) in enumerate(sides):
        pltpu.make_async_copy(tile, dst.at[pl.ds(0, B - AB), pl.ds(0, 16), :], tsem.at[e]).wait()


def solution(mesh):
    def local_step(hidden, cache_lens, k_cache, v_cache, ln_gain, ln_bias, w_query, b_query, w_kv, b_kv, w_out, b_out):
        hbm = pl.BlockSpec(memory_space=pltpu.HBM)
        vm = pl.BlockSpec(memory_space=pltpu.VMEM)
        smem = pl.BlockSpec(memory_space=pltpu.SMEM)
        sem = pltpu.SemaphoreType.DMA

        def pin(*arrays):
            return [pltpu.with_memory_space_constraint(a, pltpu.VMEM) for a in arrays]

        def far(*arrays):
            return [pltpu.with_memory_space_constraint(a, pltpu.HBM) for a in arrays]

        cache = jax.ShapeDtypeStruct((B, T, DH), BF16)
        q3, kv, o0, lse0, k_part, v_part = pl.pallas_call(
            first_kernel,
            out_shape=(pltpu.VMEM((B * H, DH), F32), pltpu.VMEM((2 * B, DH), F32), pltpu.VMEM((AB * H, DH), F32), pltpu.VMEM((AB // CS * H, DH), F32), cache, cache),
            in_specs=[smem, hbm, hbm, hbm, vm, vm, hbm, vm, hbm, vm],
            out_specs=(vm, vm, vm, vm, hbm, hbm),
            scratch_shapes=[
                pltpu.VMEM((B, D), BF16), pltpu.VMEM((B, D), BF16), pltpu.VMEM((D, H * DH), BF16), pltpu.VMEM((D, 2 * DH), BF16),
                pltpu.VMEM((AB, T, DH), BF16), pltpu.VMEM((AB, T, DH), BF16), *STAGE_BUFS, sem((NQ + 3,)), sem((4,)),
            ],
            compiler_params=pltpu.CompilerParams(vmem_limit_bytes=33 * MIB),
            name="first",
        )(*far(cache_lens, hidden, k_cache, v_cache, ln_gain[None], ln_bias[None], w_query, b_query[None], w_kv, b_kv[None]))
        held = pltpu.VMEM((2 * (B - AB), T, DH), BF16)
        y, kv_held = pl.pallas_call(
            exchange_kernel,
            out_shape=(pltpu.VMEM((B, D), F32), held),
            in_specs=[smem, vm, vm, vm, vm, hbm, hbm, hbm],
            out_specs=(vm, vm),
            scratch_shapes=[
                pltpu.VMEM((H * DH, DC), BF16), pltpu.VMEM((B * H, DH), F32), pltpu.VMEM((NC * H, DH), F32), *STAGE_BUFS,
                pltpu.VMEM((NC, 2, S * H, DH), F32), pltpu.VMEM((NC, H, DH), F32),
                pltpu.VMEM((NC, 2, S * H, DH), F32), pltpu.VMEM((NC, H, DH), F32),
                pltpu.VMEM((NC, S * H, DH), F32), pltpu.VMEM((NC, H, DH), F32),
                pltpu.VMEM((NC, R * H, DH), F32), pltpu.VMEM((NC, R, DC), F32), pltpu.VMEM((NC, R, DY), F32),
                sem, sem((2 * (B // AB) - 2,)), sem((NC, 3)), sem((NC, 3)), sem((NC, 2)), sem((NC, 2)), sem((NC,)), sem((NC,)),
                sem((NC,)), sem((NC,)), sem((NC, 4)), sem((NC, 4)), sem((NC, 4)), sem((NC, 4)),
            ],
            compiler_params=pltpu.CompilerParams(vmem_limit_bytes=24 * MIB, collective_id=0, has_side_effects=True),
            name="exchange",
        )(*far(cache_lens), *pin(q3, kv, o0, lse0), *far(k_cache, v_cache, w_out))
        k_new, v_new, out_hidden = pl.pallas_call(
            last_kernel,
            out_shape=(cache, cache, jax.ShapeDtypeStruct((B, D), BF16)),
            in_specs=[smem, vm, vm, vm, vm, vm, hbm, hbm],
            out_specs=(hbm, hbm, hbm),
            input_output_aliases={6: 0, 7: 1},
            scratch_shapes=[pltpu.VMEM((B - AB, 16, DH), BF16), pltpu.VMEM((B - AB, 16, DH), BF16), pltpu.VMEM((B, D), BF16),
                            sem((2 * (B // AB) - 2,)), sem, sem((2,))],
            compiler_params=pltpu.CompilerParams(vmem_limit_bytes=6 * MIB),
            name="last",
        )(*far(cache_lens), *pin(kv, y), hidden, b_out[None], *pin(kv_held), k_part, v_part)
        return out_hidden, k_new, v_new

    cache_spec = P("dp", "sq", None)
    row_spec = P("dp", None)
    in_specs = (row_spec, P("dp"), cache_spec, cache_spec, P(None), P(None), P(None, "tp"), P("tp"), P(None, None), P(None), P("tp", None), P(None))
    out_specs = (row_spec, cache_spec, cache_spec)
    return jax.shard_map(local_step, mesh=mesh, in_specs=in_specs, out_specs=out_specs, check_vma=False)
```

time: 78.4 us -> 76 us (0.969)
  Pallas kernels: 77.4 us -> 74.9 us
    pallas_call x1, Pallas kernels: 52.3 us -> 48.8 us  [local_step(): pl.pallas_call(exchange_kernel, out_shape=(pltpu.VMEM((B, D), F32), held)...]
    pallas_call x1, Pallas kernels: 9.77 us -> 11.1 us  [local_step(): pl.pallas_call(last_kernel, out_shape=(cache, cache, jax.ShapeDtypeStruct...]
where the time goes in v4:
time: 76 us; the launch traced here: 75.8 us
  Pallas kernels  74.9 us (99%)
  between operations  0.84 us (1%)
    pallas_call x1, Pallas kernels, local_step(): pl.pallas_call(exchange_kernel, out_shape=(pltpu.VMEM((B, D), F32), held)...  48.8 us
    pallas_call x1, Pallas kernels, local_step(): pl.pallas_call(first_kernel, out_shape=(pltpu.VMEM((B * H, DH), F32), plt...  15.1 us
    pallas_call x1, Pallas kernels, local_step(): pl.pallas_call(last_kernel, out_shape=(cache, cache, jax.ShapeDtypeStruct...  11.1 us

profile of v4, /device:TPU:0, one launch (start us, length us, event | category | flops | bytes accessed | tf_op | source)
XLA Modules:
  0.0 75.8 jit_solution(5786779230591485669)
XLA Ops:
  0.6 15.1 %first.1 = (f32[4096,128]{1,0:T(8,128)S(1)}, f32[512,128]{1,0:T(8,128)S(1)}, f32[1024,128]{1,0:T(8,128)S(1)}, f32[32,128]{1,0:T(8,128)S(1)}, bf16[256,256,128]{2...) custom-call(s32[256]{0:T(256)} %lens.5, bf16[256,4096]{1,0:T(8,128)(2,1)} %hid.1, bf16[256,256,128]{2,1,0:T(8,128)(2,1)} %k_hbm.3, ...), custom_call_target="tpu_custom_call" | custom-call | tf_op jit(solution)/shard_map/first/pallas_call | solution.py:388
  15.7 0.0 copy-start
  15.7 0.0 copy-start.1
  15.7 48.8 %exchange.1 = (f32[256,4096]{1,0:T(8,128)S(1)}, bf16[384,256,128]{2,1,0:T(8,128)(2,1)S(1)}) custom-call(s32[256]{0:T(256)} %lens.5, f32[4096,128]{1,0:T(8,128)S(1)} %get-tuple-element.15.q3, f32[512,128]{1,0:T(8,128)S(1)} %get-tuple-element.14.kv, f32[1024,128]{1,0:T(8,128)S(1)} %get-tuple-element.16.o_first, f32[32,128]{1,0:T(8,128)S(1)} %get-tuple-element.17.lse_first, ...), custom_call_target="tpu_custom_call" | custom-call | tf_op jit(solution)/shard_map/exchange/pallas_call | solution.py:401
  64.5 0.0 copy-done
  64.5 0.0 copy-done.1
  64.5 11.1 %last.1 = (bf16[256,256,128]{2,1,0:T(8,128)(2,1)}, bf16[256,256,128]{2,1,0:T(8,128)(2,1)}, bf16[256,4096]{1,0:T(8,128)(2,1)}) custom-call(s32[256]{0:T(256)} %lens.5, f32[512,128]{1,0:T(8,128)S(1)} %get-tuple-element.14.kv, f32[256,4096]{1,0:T(8,128)S(1)} %get-tuple-element.18.y_in, ...), custom_call_target="tpu_custom_call", output_to_operand_aliasing={{0}: (6, {}), {1}: (7, {})} | custom-call | tf_op jit(solution)/shard_map/last/pallas_call | solution.py:418
Async XLA Ops:
  15.7 48.8 %copy-start = (bf16[256,4096]{1,0:T(8,128)(2,1)S(1)}, bf16[256,4096]{1,0:T(8,128)(2,1)}, u32[]{:S(2)}) copy-start(bf16[256,4096]{1,0:T(8,128)(2,1)} %hid.1) | copy-start | bytes 6291460
  15.7 48.8 %copy-start.1 = (f32[4096]{0:T(1024)S(1)}, f32[4096]{0:T(1024)}, u32[]{:S(2)}) copy-start(f32[4096]{0:T(1024)} %param.23) | copy-start | bytes 49156

commit v5 on v4

--- a/solution.py
+++ b/solution.py
@@ -126,25 +126,31 @@
     lax.fori_loop(lo, hi, insert, 0, unroll=4)
 
 
-def first_kernel(lens, hid_hbm, k_hbm, v_hbm, gain_ref, bias_ref, wq_hbm, bq_ref, wkv_hbm, bkv_ref,
+def first_kernel(lens_hbm, hid_hbm, k_hbm, v_hbm, gain_hbm, bias_hbm, wq_hbm, bq_hbm, wkv_hbm, bkv_hbm,
                  q3, kv, o_ref, lse_ref, ko_hbm, vo_hbm,
-                 hid, h, wq, wkv, kbuf, vbuf, b0, b1, b2, b3, b4, b5, b6, b7, wsem, csem):
+                 lens, gain_ref, bias_ref, bq_ref, bkv_ref, hid, h, wq, wkv, kbuf, vbuf, b0, b1, b2, b3, b4, b5, b6, b7, wsem, csem, ssem):
     first = lax.axis_index("sq") * T
+    small = [pltpu.make_async_copy(src, dst, ssem.at[e]) for e, (src, dst) in enumerate((
+        (gain_hbm, gain_ref), (bias_hbm, bias_ref), (bkv_hbm, bkv_ref), (bq_hbm, bq_ref), (lens_hbm, lens)))]
     load_h = []
     for e in range(2):
         rows = pl.ds(e * (B // 2), B // 2)
         load_h.append(pltpu.make_async_copy(hid_hbm.at[rows], hid.at[rows], wsem.at[NQ + e]))
         load_h[-1].start()
+        if e == 0:
+            for cp in small:
+                cp.start()
     load_wkv = pltpu.make_async_copy(wkv_hbm, wkv, wsem.at[NQ + 2])
     load_wkv.start()
     load_wq = []
     for j in range(NQ):
         cols = pl.ds(j * QB, QB)
         load_wq.append(pltpu.make_async_copy(wq_hbm.at[:, cols], wq.at[:, cols], wsem.at[j]))
-        load_wq[-1].start()
     loads = [pltpu.make_async_copy(src.at[pl.ds(0, AB)], dst, csem.at[e]) for e, (src, dst) in enumerate(((k_hbm, kbuf), (v_hbm, vbuf)))]
-    for c in loads:
-        c.start()
+    for cp in [*load_wq[:-1], *loads, load_wq[-1]]:
+        cp.start()
+    small[0].wait()
+    small[1].wait()
 
     def norm_rows(i, _):
         rows = pl.ds(pl.multiple_of(i * 16, 16), 16)
@@ -160,22 +166,28 @@
         load_h[e].wait()
         lax.fori_loop(e * (B // 32), (e + 1) * (B // 32), norm_rows, 0, unroll=2)
     load_wkv.wait()
+    for cp in small[2:]:
+        cp.wait()
+    load_wq[0].wait()
     new_kv = (jnp.dot(h[...], wkv[...], preferred_element_type=F32) + bkv_ref[...]).astype(BF16).astype(F32)
     kv[0:B, :] = new_kv[:, :DH]
     kv[B:2 * B, :] = new_kv[:, DH:]
+    stores = [pltpu.make_async_copy(src, dst.at[pl.ds(0, AB)], csem.at[2 + e]) for e, (src, dst) in enumerate(((kbuf, ko_hbm), (vbuf, vo_hbm)))]
     for j in range(NQ):
-        load_wq[j].wait()
         cols = pl.ds(j * QB, QB)
         q = jnp.dot(h[...], wq[:, cols], preferred_element_type=F32) + bq_ref[:, cols]
         q = q.astype(BF16).astype(F32)
+        if j < NQ - 2:
+            load_wq[j + 1].wait()
         for n in range(QB // DH):
             q3[pl.ds(j * (QB // DH) + n, B, stride=H), :] = q[:, n * DH:(n + 1) * DH]
-    for c in loads:
-        c.wait()
-    insert_rows(lens, first, kv, (kbuf, vbuf), 0, AB, 0)
-    stores = [pltpu.make_async_copy(src, dst.at[pl.ds(0, AB)], csem.at[2 + e]) for e, (src, dst) in enumerate(((kbuf, ko_hbm), (vbuf, vo_hbm)))]
-    for c in stores:
-        c.start()
+        if j == NQ - 2:
+            for c in loads:
+                c.wait()
+            insert_rows(lens, first, kv, (kbuf, vbuf), 0, AB, 0)
+            for c in stores:
+                c.start()
+            load_wq[j + 1].wait()
     attention_stages(lens, first, q3, kbuf, vbuf, 0, 0, kv, o_ref, lse_ref, (b0, b1, b2, b3, b4, b5, b6, b7))(0)
     for c in stores:
         c.wait()
@@ -192,15 +204,20 @@
     return wa / tot, wb / tot, top + jnp.log2(tot)
 
 
-def exchange_kernel(lens, q3, kv, o_first, lse_first, k_hbm, v_hbm, wo_hbm, y_ref, held,
-                    wo, o_ref, lse_ref, b0, b1, b2, b3, b4, b5, b6, b7, o_core, l_core, o_mix, l_mix, o_x, l_x, a_all, part, p_y,
-                    wsem, csem, a0s, a0r, a1s, a1r, a2s, a2r, bs, br, cs, cr, ds, dr):
+def exchange_kernel(lens_hbm, q3, kv, o_first, lse_first, k_hbm, v_hbm, wo_hbm, y_ref, held,
+                    lens, wo, o_ref, lse_ref, b0, b1, b2, b3, b4, b5, b6, b7, o_core, l_core, o_mix, l_mix, l_half, o_x, l_x, a_all, part, p_y,
+                    wsem, csem, nsem, a0s, a0r, a1s, a1r, a2s, a2r, bs, br, cs, cr, ds, dr):
     sq, tp = lax.axis_index("sq"), lax.axis_index("tp")
     x, c = sq // 2, sq % 2
     mate = {"sq": x * 2 + 1 - c}
     over_x = {"sq": (1 - x) * 2 + c}
     over_y = {"tp": 1 - tp}
     loads = {}
+    bar = pltpu.get_barrier_semaphore()
+    for dev in (mate, over_x, over_y):
+        pl.semaphore_signal(bar, inc=1, device_id=dev, device_id_type=MESH)
+    load_lens = pltpu.make_async_copy(lens_hbm, lens, nsem)
+    load_lens.start()
 
     def fetch(k):
         rows = pl.ds(k * AB, AB)
@@ -214,9 +231,7 @@
     load = pltpu.make_async_copy(wo_hbm.at[:, pl.ds(pl.multiple_of(c * DC, DC), DC)], wo, wsem)
     load.start()
     fetch(3)
-    bar = pltpu.get_barrier_semaphore()
-    for dev in (mate, over_x, over_y):
-        pl.semaphore_signal(bar, inc=1, device_id=dev, device_id_type=MESH)
+    load_lens.wait()
     pl.semaphore_wait(bar, 3)
 
     def send(src, dst, ssem, rsem, dev):
@@ -228,6 +243,7 @@
     hop0, hop1, hop2, hopb, hopc, hopd = {}, {}, {}, {}, {}, {}
     stages = attention_stages(lens, sq * T, q3, held, held, AB, AB - (B - AB), kv, o_ref, lse_ref, (b0, b1, b2, b3, b4, b5, b6, b7))
     ready = []
+    lane8 = lax.broadcasted_iota(jnp.int32, (H // 2, DH), 1)
 
     def attend(k):
         block = k * CS // AB
@@ -253,6 +269,8 @@
         shift = lax.rem(DH - c * S, DH)
         fa, fb, lm = merge(pltpu.roll(l_k[pl.ds(k * H, H), :], shift, 1), pltpu.roll(l_core[k], shift, 1))
         l_mix[k] = lm
+        theirs = pltpu.roll(lm, lax.rem(DH - (1 - x) * R, DH), 1)
+        l_half[k] = jnp.where(lane8 < S, theirs[:H // 2], pltpu.roll(theirs[H // 2:], S, 1))
         for xx in range(2):
             mine = (k * 4 + xx * 2 + c) * W
             for j in range(S):
@@ -261,13 +279,14 @@
                 at = xx * R + j
                 o_mix[k, xx, j * H:(j + 1) * H, :] = column(fa, at) * oa + column(fb, at) * ob
         hop1[k] = [send(o_mix.at[k, 1 - x], o_x.at[k], a1s.at[k, 0], a1r.at[k, 0], over_x),
-                   send(l_mix.at[k], l_x.at[k], a1s.at[k, 1], a1r.at[k, 1], over_x)]
+                   send(l_half.at[k], l_x.at[k], a1s.at[k, 1], a1r.at[k, 1], over_x)]
 
     def quarter(k):
         for cp in hop1[k]:
             cp.wait_recv()
         shift = lax.rem(DH - x * R, DH)
-        fa, fb, _ = merge(pltpu.roll(l_mix[k], shift, 1), pltpu.roll(l_x[k], shift, 1))
+        l_far = jnp.concatenate([l_x[k], pltpu.roll(l_x[k], DH - S, 1)], 0)
+        fa, fb, _ = merge(pltpu.roll(l_mix[k], shift, 1), l_far)
         for j in range(S):
             oa = o_mix[k, x, j * H:(j + 1) * H, :]
             ob = o_x[k, j * H:(j + 1) * H, :]
@@ -320,55 +339,35 @@
             cp.wait_send()
 
 
-def last_kernel(lens, kv, y_in, hid, bo_ref, held, k_part, v_part, ko_hbm, vo_hbm, out_hbm, ktile, vtile, out, sem, osem, tsem):
-    first = lax.axis_index("sq") * T
-    sub = lax.broadcasted_iota(jnp.int32, (16, DH), 0)
-    sides = ((0, ktile, ko_hbm), (B - AB, vtile, vo_hbm))
-    blocks = range(1, B // AB)
-    copies = {}
-    for k in blocks:
-        for e, (src, _, dst) in enumerate(sides):
-            copies[k, e] = pltpu.make_async_copy(held.at[pl.ds(src + (k - 1) * AB, AB)], dst.at[pl.ds(k * AB, AB)], sem.at[2 * k + e - 2])
-            copies[k, e].start()
+def last_kernel(lens_hbm, kv, y_in, hid, bo_ref, held_in, k_part, v_part, ko_hbm, vo_hbm, out_hbm, held, lens, out, sem, osem):
+    load_lens = pltpu.make_async_copy(lens_hbm, lens, osem)
+    load_lens.start()
 
     def rows(i, _):
         r = pl.ds(pl.multiple_of(i * 16, 16), 16)
         out[r, :] = (hid[r, :].astype(F32) + y_in[r, :] + bo_ref[...]).astype(BF16)
         return 0
 
-    lax.fori_loop(0, B // 16, rows, 0, unroll=2)
-    store_out = pltpu.make_async_copy(out, out_hbm, osem)
-    store_out.start()
-
-    def spot(b):
-        row = lens[b] - first
-        start = pl.multiple_of((jnp.clip(row, 0, T - 1) // 16) * 16, 16)
-        return row, start
-
-    def build(b, _):
-        row, start = spot(b)
-        hit = sub == row - start
-        for c, (src, tile, _) in enumerate(sides):
-            new = kv[pl.ds(c * B + b, 1), :]
-            old = held[b - AB + src, pl.ds(start, 16), :].astype(F32)
-            tile[b - AB] = jnp.where(hit, new, old).astype(BF16)
-        return 0
-
-    lax.fori_loop(AB, B, build, 0, unroll=4)
-
-    def put(b, _):
-        _, start = spot(b)
-        for e, (_, tile, dst) in enumerate(sides):
-            pltpu.make_async_copy(tile.at[b - AB], dst.at[b, pl.ds(start, 16), :], tsem.at[e]).start()
-        return 0
-
-    for k in blocks:
-        for e in range(2):
-            copies[k, e].wait()
-        lax.fori_loop(k * AB, (k + 1) * AB, put, 0, unroll=4)
-    store_out.wait()
-    for e, (_, tile, dst) in enumerate(sides):
-        pltpu.make_async_copy(tile, dst.at[pl.ds(0, B - AB), pl.ds(0, 16), :], tsem.at[e]).wait()
+    lax.fori_loop(0, B // 32, rows, 0, unroll=2)
+    load_lens.wait()
+    first = lax.axis_index("sq") * T
+    n = B - AB
+    copies = []
+
+    def put(k):
+        insert_rows(lens, first, kv, (held.at[pl.ds(0, n)], held.at[pl.ds(n, n)]), k * AB, (k + 1) * AB, AB)
+        for e, dst in enumerate((ko_hbm, vo_hbm)):
+            copies.append(pltpu.make_async_copy(held.at[pl.ds(e * n + (k - 1) * AB, AB)], dst.at[pl.ds(k * AB, AB)], sem.at[2 * k + e - 2]))
+            copies[-1].start()
+
+    put(1)
+    lax.fori_loop(B // 32, B // 16, rows, 0, unroll=2)
+    copies.append(pltpu.make_async_copy(out, out_hbm, osem))
+    copies[-1].start()
+    for k in range(2, B // AB):
+        put(k)
+    for cp in copies:
+        cp.wait()
 
 
 def solution(mesh):
@@ -388,11 +387,12 @@
         q3, kv, o0, lse0, k_part, v_part = pl.pallas_call(
             first_kernel,
             out_shape=(pltpu.VMEM((B * H, DH), F32), pltpu.VMEM((2 * B, DH), F32), pltpu.VMEM((AB * H, DH), F32), pltpu.VMEM((AB // CS * H, DH), F32), cache, cache),
-            in_specs=[smem, hbm, hbm, hbm, vm, vm, hbm, vm, hbm, vm],
+            in_specs=[hbm] * 10,
             out_specs=(vm, vm, vm, vm, hbm, hbm),
             scratch_shapes=[
+                pltpu.SMEM((B,), jnp.int32), pltpu.VMEM((1, D), F32), pltpu.VMEM((1, D), F32), pltpu.VMEM((1, H * DH), F32), pltpu.VMEM((1, 2 * DH), F32),
                 pltpu.VMEM((B, D), BF16), pltpu.VMEM((B, D), BF16), pltpu.VMEM((D, H * DH), BF16), pltpu.VMEM((D, 2 * DH), BF16),
-                pltpu.VMEM((AB, T, DH), BF16), pltpu.VMEM((AB, T, DH), BF16), *STAGE_BUFS, sem((NQ + 3,)), sem((4,)),
+                pltpu.VMEM((AB, T, DH), BF16), pltpu.VMEM((AB, T, DH), BF16), *STAGE_BUFS, sem((NQ + 3,)), sem((4,)), sem((5,)),
             ],
             compiler_params=pltpu.CompilerParams(vmem_limit_bytes=33 * MIB),
             name="first",
@@ -401,28 +401,28 @@
         y, kv_held = pl.pallas_call(
             exchange_kernel,
             out_shape=(pltpu.VMEM((B, D), F32), held),
-            in_specs=[smem, vm, vm, vm, vm, hbm, hbm, hbm],
+            in_specs=[hbm, vm, vm, vm, vm, hbm, hbm, hbm],
             out_specs=(vm, vm),
             scratch_shapes=[
+                pltpu.SMEM((B,), jnp.int32),
                 pltpu.VMEM((H * DH, DC), BF16), pltpu.VMEM((B * H, DH), F32), pltpu.VMEM((NC * H, DH), F32), *STAGE_BUFS,
                 pltpu.VMEM((NC, 2, S * H, DH), F32), pltpu.VMEM((NC, H, DH), F32),
-                pltpu.VMEM((NC, 2, S * H, DH), F32), pltpu.VMEM((NC, H, DH), F32),
-                pltpu.VMEM((NC, S * H, DH), F32), pltpu.VMEM((NC, H, DH), F32),
+                pltpu.VMEM((NC, 2, S * H, DH), F32), pltpu.VMEM((NC, H, DH), F32), pltpu.VMEM((NC, H // 2, DH), F32),
+                pltpu.VMEM((NC, S * H, DH), F32), pltpu.VMEM((NC, H // 2, DH), F32),
                 pltpu.VMEM((NC, R * H, DH), F32), pltpu.VMEM((NC, R, DC), F32), pltpu.VMEM((NC, R, DY), F32),
-                sem, sem((2 * (B // AB) - 2,)), sem((NC, 3)), sem((NC, 3)), sem((NC, 2)), sem((NC, 2)), sem((NC,)), sem((NC,)),
+                sem, sem((2 * (B // AB) - 2,)), sem, sem((NC, 3)), sem((NC, 3)), sem((NC, 2)), sem((NC, 2)), sem((NC,)), sem((NC,)),
                 sem((NC,)), sem((NC,)), sem((NC, 4)), sem((NC, 4)), sem((NC, 4)), sem((NC, 4)),
             ],
             compiler_params=pltpu.CompilerParams(vmem_limit_bytes=24 * MIB, collective_id=0, has_side_effects=True),
             name="exchange",
         )(*far(cache_lens), *pin(q3, kv, o0, lse0), *far(k_cache, v_cache, w_out))
-        k_new, v_new, out_hidden = pl.pallas_call(
+        k_new, v_new, out_hidden, _ = pl.pallas_call(
             last_kernel,
-            out_shape=(cache, cache, jax.ShapeDtypeStruct((B, D), BF16)),
-            in_specs=[smem, vm, vm, vm, vm, vm, hbm, hbm],
-            out_specs=(hbm, hbm, hbm),
-            input_output_aliases={6: 0, 7: 1},
-            scratch_shapes=[pltpu.VMEM((B - AB, 16, DH), BF16), pltpu.VMEM((B - AB, 16, DH), BF16), pltpu.VMEM((B, D), BF16),
-                            sem((2 * (B // AB) - 2,)), sem, sem((2,))],
+            out_shape=(cache, cache, jax.ShapeDtypeStruct((B, D), BF16), held),
+            in_specs=[hbm, vm, vm, vm, vm, vm, hbm, hbm],
+            out_specs=(hbm, hbm, hbm, vm),
+            input_output_aliases={5: 3, 6: 0, 7: 1},
+            scratch_shapes=[pltpu.SMEM((B,), jnp.int32), pltpu.VMEM((B, D), BF16), sem((2 * (B // AB) - 2,)), sem],
             compiler_params=pltpu.CompilerParams(vmem_limit_bytes=6 * MIB),
             name="last",
         )(*far(cache_lens), *pin(kv, y), hidden, b_out[None], *pin(kv_held), k_part, v_part)

time: 76 us -> 74 us (0.974)
  Pallas kernels: 74.9 us -> 73 us
where the time goes in v5:
time: 74 us; the launch traced here: 73.9 us
  Pallas kernels  73 us (99%)
  between operations  0.84 us (1%)
    pallas_call x1, Pallas kernels, local_step(): pl.pallas_call(exchange_kernel, out_shape=(pltpu.VMEM((B, D), F32), held)...  48.1 us
    pallas_call x1, Pallas kernels, local_step(): pl.pallas_call(first_kernel, out_shape=(pltpu.VMEM((B * H, DH), F32), plt...  14.5 us
    pallas_call x1, Pallas kernels, local_step(): pl.pallas_call(last_kernel, out_shape=(cache, cache, jax.ShapeDtypeStruct...  10.4 us

profile of v5, /device:TPU:0, one launch (start us, length us, event | category | flops | bytes accessed | tf_op | source)
XLA Modules:
  0.0 73.9 jit_solution(5218243139697725294)
XLA Ops:
  0.6 14.5 %first.1 = (f32[4096,128]{1,0:T(8,128)S(1)}, f32[512,128]{1,0:T(8,128)S(1)}, f32[1024,128]{1,0:T(8,128)S(1)}, f32[32,128]{1,0:T(8,128)S(1)}, bf16[256,256,128]{2...) custom-call(s32[256]{0:T(256)} %lens_hbm.5, bf16[256,4096]{1,0:T(8,128)(2,1)} %hid.1, bf16[256,256,128]{2,1,0:T(8,128)(2,1)} %k_hbm.3, ...), custom_call_target="tpu_custom_call" | custom-call | tf_op jit(solution)/shard_map/first/pallas_call | solution.py:387
  15.1 0.0 copy-start
  15.2 0.0 copy-start.1
  15.2 48.1 %exchange.1 = (f32[256,4096]{1,0:T(8,128)S(1)}, bf16[384,256,128]{2,1,0:T(8,128)(2,1)S(1)}) custom-call(s32[256]{0:T(256)} %lens_hbm.5, f32[4096,128]{1,0:T(8,128)S(1)} %get-tuple-element.15.q3, f32[512,128]{1,0:T(8,128)S(1)} %get-tuple-element.14.kv, f32[1024,128]{1,0:T(8,128)S(1)} %get-tuple-element.16.o_first, f32[32,128]{1,0:T(8,128)S(1)} %get-tuple-element.17.lse_first, ...), custom_call_target="tpu_custom_call" | custom-call | tf_op jit(solution)/shard_map/exchange/pallas_call | solution.py:401
  63.3 0.0 copy-done
  63.3 0.0 copy-done.1
  63.3 10.4 %last.1 = (bf16[256,256,128]{2,1,0:T(8,128)(2,1)}, bf16[256,256,128]{2,1,0:T(8,128)(2,1)}, bf16[256,4096]{1,0:T(8,128)(2,1)}, bf16[384,256,128]{2,1,0:T(8,128)(2,1)S(1)}) custom-call(s32[256]{0:T(256)} %lens_hbm.5, f32[512,128]{1,0:T(8,128)S(1)} %get-tuple-element.14.kv, ...), custom_call_target="tpu_custom_call", output_to_operand_aliasing={{3}: (5, {}), {0}: (6, {}), {1}: (7, {})} | custom-call | tf_op jit(solution)/shard_map/last/pallas_call | solution.py:419
Async XLA Ops:
  15.1 48.2 %copy-start = (bf16[256,4096]{1,0:T(8,128)(2,1)S(1)}, bf16[256,4096]{1,0:T(8,128)(2,1)}, u32[]{:S(2)}) copy-start(bf16[256,4096]{1,0:T(8,128)(2,1)} %hid.1) | copy-start | bytes 6291460
  15.2 48.2 %copy-start.1 = (f32[4096]{0:T(1024)S(1)}, f32[4096]{0:T(1024)}, u32[]{:S(2)}) copy-start(f32[4096]{0:T(1024)} %param.23) | copy-start | bytes 49156

commit v6 on v5

v6 whole, which is shorter than its diff:
```python
import functools
import math

import jax
import jax.numpy as jnp
from jax import lax
from jax.experimental import pallas as pl
from jax.experimental.pallas import tpu as pltpu
from jax.sharding import PartitionSpec as P

MESH = pl.DeviceIdType.MESH
F32 = jnp.float32
BF16 = jnp.bfloat16
NEG = -1e30
B = 256
D = 4096
H = 16
DH = 128
T = 256
AB = 64
NC = 8
CS = B // NC
S = CS // 4
R = 2 * S
DC = D // 2
DY = DC // 2
QB = 512
HC = H // 2
NQ = HC * DH // QB
QSCALE = DH ** -0.5 * math.log2(math.e)
GROUP = 8
MIB = 1024 * 1024
MLIM = 24 * MIB
VIA_Y = 256
SCHEDULE = [(s[0], int(s[1])) for s in (
    "a0", "s0", "s1", "a2", "m0", "s2", "m1", "a4", "m2", "q0", "s5", "a6", "m5", "s3", "q1", "s7", "s4", "p0", "q2", "s6", "m3", "p1", "m4", "p2", "m6", "q5", "f0", "q3", "m7", "q4", "f1", "p3", "p4", "q6", "r0", "p5", "q7", "f2", "p6", "r1", "p7", "f4", "f3", "f5", "l0", "f6", "f7", "r2", "r3", "r4", "r5", "r6", "r7", "l1", "l2", "l3", "l4", "l5", "l6", "l7")]
def attention_stages(lens, first, q2, held, kv, o_ref, lse_ref, bufs):
    lane = lax.broadcasted_iota(jnp.int32, (H, DH), 1)
    pos = lax.broadcasted_iota(jnp.int32, (H, T), 1)
    zero = jnp.zeros((H, DH), BF16)
    s_a, s_b, p_a, p_b, r_a, r_b, n_a, n_b = bufs

    def query(b):
        rows = pl.ds(pl.multiple_of(b * HC, HC), HC)
        return jnp.concatenate([q2[0, rows, :], q2[1, rows, :]], 0)

    def score(i, s_out):
        for u in range(0, GROUP, 2):
            b = i * GROUP + u
            q0 = query(b).astype(BF16)
            q1 = query(b + 1).astype(BF16)
            lhs = jnp.concatenate([jnp.concatenate([q0, zero], 1), jnp.concatenate([zero, q1], 1)], 0)
            keys = jnp.concatenate([held[b], held[b + 1]], 1)
            s_out[u * H:(u + 2) * H, :] = lax.dot_general(lhs, keys, (((1,), (1,)), ((), ())), preferred_element_type=F32)

    def soften(i, s_in, p_out, r_out, n_out):
        chunk = lax.div(i * GROUP, CS)
        tile = pl.ds(pl.multiple_of(chunk * H, H), H)
        at = i * GROUP - chunk * CS
        lses = lse_ref[tile, :]
        for u in range(GROUP):
            b = i * GROUP + u
            row = lens[b] - first
            here = jnp.logical_and(row >= 0, row < T)
            k_new = kv[pl.ds(b, 1), :]
            v_new = kv[pl.ds(B + b, 1), :]
            q_row = query(b)
            s_new = jnp.where(here, jnp.sum(q_row * k_new, axis=1, keepdims=True) * QSCALE, NEG)
            se = jnp.where(pos < row, s_in[u * H:(u + 1) * H, :] * QSCALE, NEG)
            m = jnp.maximum(jnp.max(se, axis=1, keepdims=True), s_new)
            p = jnp.exp2(se - m)
            p_new = jnp.exp2(s_new - m)
            l = jnp.sum(p, axis=1, keepdims=True) + p_new
            r = 1.0 / l
            p_out[u * H:(u + 1) * H, :] = p.astype(BF16)
            r_out[u * H:(u + 1) * H, :] = jnp.broadcast_to(r, (H, DH))
            n_out[u * H:(u + 1) * H, :] = (p_new * r) * v_new
            lses = jnp.where(lane == at + u, m + jnp.log2(l), lses)
        lse_ref[tile, :] = lses

    def weigh(i, p_in, r_in, n_in):
        for u in range(0, GROUP, 2):
            b = i * GROUP + u
            vals = jnp.concatenate([held[B + b], held[B + b + 1]], 1)
            o = jnp.dot(p_in[u * H:(u + 2) * H, :], vals, preferred_element_type=F32)
            for e in range(2):
                part = slice((u + e) * H, (u + e + 1) * H)
                o_ref[pl.ds(pl.multiple_of((b + e) * H, H), H), :] = (
                    o[e * H:(e + 1) * H, e * DH:(e + 1) * DH] * r_in[part, :] + n_in[part, :])

    def attend(k):
        tiles = slice(k * AB // CS * H, (k + 1) * AB // CS * H)
        lse_ref[tiles, :] = jnp.zeros((AB // CS * H, DH), F32)
        lo, hi = k * AB // GROUP, (k + 1) * AB // GROUP
        score(lo, s_a)
        score(lo + 1, s_b)
        soften(lo, s_a, p_a, r_a, n_a)

        def body(t, _):
            i = lo + 2 + 2 * t
            score(i, s_a)
            soften(i - 1, s_b, p_b, r_b, n_b)
            weigh(i - 2, p_a, r_a, n_a)
            score(i + 1, s_b)
            soften(i, s_a, p_a, r_a, n_a)
            weigh(i - 1, p_b, r_b, n_b)
            return 0

        lax.fori_loop(0, (hi - lo - 2) // 2, body, 0)
        soften(hi - 1, s_b, p_b, r_b, n_b)
        weigh(hi - 2, p_a, r_a, n_a)
        weigh(hi - 1, p_b, r_b, n_b)

    return attend


STAGE_BUFS = [pltpu.VMEM((GROUP * H, T), F32)] * 2 + [pltpu.VMEM((GROUP * H, T), BF16)] * 2 + [pltpu.VMEM((GROUP * H, DH), F32)] * 4


def insert_rows(lens, first, kv, held, lo, hi):
    sub = lax.broadcasted_iota(jnp.int32, (16, DH), 0)

    def insert(b, _):
        row = lens[b] - first
        start = pl.multiple_of((jnp.clip(row, 0, T - 1) // 16) * 16, 16)
        hit = sub == row - start
        for c in range(2):
            new = kv[pl.ds(c * B + b, 1), :]
            old = held[c * B + b, pl.ds(start, 16), :].astype(F32)
            held[c * B + b, pl.ds(start, 16), :] = jnp.where(hit, new, old).astype(BF16)
        return 0

    lax.fori_loop(lo, hi, insert, 0, unroll=4)


def column(tile, j):
    return tile[:, j:j + 1]


def merge(la, lb):
    top = jnp.maximum(la, lb)
    wa, wb = jnp.exp2(la - top), jnp.exp2(lb - top)
    tot = wa + wb
    return wa / tot, wb / tot, top + jnp.log2(tot)


def step_kernel(lens_hbm, hid_hbm, k_hbm, v_hbm, gain_hbm, bias_hbm, wq_hbm, bq_hbm, wkv_hbm, bkv_hbm, wo_hbm,
                y_ref, held, kv,
                lens, gain_ref, bias_ref, bq_ref, bkv_ref, h, w, wkv, q2, o_ref, lse_ref, b0, b1, b2, b3, b4, b5, b6, b7,
                o_core, l_core, o_mix, l_mix, l_half, o_x, l_x, a_all, part, p_y,
                hsem, ssem, wsem, csem, qs, qr, a0s, a0r, a1s, a1r, a2s, a2r, bs, br, cs, cr, ds, dr):
    sq, tp = lax.axis_index("sq"), lax.axis_index("tp")
    x, c = sq // 2, sq % 2
    mate = {"sq": x * 2 + 1 - c}
    over_x = {"sq": (1 - x) * 2 + c}
    over_y = {"tp": 1 - tp}
    bar = pltpu.get_barrier_semaphore()
    for dev in (mate, over_x, over_y):
        pl.semaphore_signal(bar, inc=1, device_id=dev, device_id_type=MESH)
    halves = [pl.ds(e * (B // 2), B // 2) for e in range(2)]
    load_h = [pltpu.make_async_copy(hid_hbm.at[halves[e]], h.at[halves[e]], hsem.at[e]) for e in range(2)]
    own_q = HC * DH
    small = [pltpu.make_async_copy(src, dst, ssem.at[e]) for e, (src, dst) in enumerate((
        (gain_hbm, gain_ref), (bias_hbm, bias_ref), (bkv_hbm, bkv_ref),
        (bq_hbm.at[:, pl.ds(pl.multiple_of(c * own_q, own_q), own_q)], bq_ref), (lens_hbm, lens)))]
    load_wkv = pltpu.make_async_copy(wkv_hbm, wkv, hsem.at[2])
    load_wq = [pltpu.make_async_copy(wq_hbm.at[:, pl.ds(pl.multiple_of(c * own_q + j * QB, QB), QB)], w.at[:, pl.ds(j * QB, QB)], wsem.at[j])
               for j in range(NQ)]
    for cp in [load_h[0], *small, load_h[1], load_wkv, *load_wq]:
        cp.start()
    loads = {}

    def fetch(k):
        loads[k] = [pltpu.make_async_copy(src.at[pl.ds(k * AB, AB)], held.at[pl.ds(e * B + k * AB, AB)], csem.at[2 * k + e])
                    for e, src in enumerate((k_hbm, v_hbm))]
        for cp in loads[k]:
            cp.start()

    fetch(0)
    fetch(1)
    small[0].wait()
    small[1].wait()

    def norm_rows(i, _):
        rows = pl.ds(pl.multiple_of(i * 16, 16), 16)
        wide = h[rows, :].astype(F32)
        mean = jnp.sum(wide, axis=-1, keepdims=True) * (1.0 / D)
        cen = wide - mean
        var = jnp.sum(cen * cen, axis=-1, keepdims=True) * (1.0 / D)
        h[rows, :] = (cen * lax.rsqrt(var + 1e-5) * gain_ref[...] + bias_ref[...]).astype(BF16)
        return 0

    for e in range(2):
        load_h[e].wait()
        lax.fori_loop(e * (B // 32), (e + 1) * (B // 32), norm_rows, 0, unroll=2)
    load_wkv.wait()
    for cp in small[2:]:
        cp.wait()
    load_wq[0].wait()
    new_kv = (jnp.dot(h[...], wkv[...], preferred_element_type=F32) + bkv_ref[...]).astype(BF16).astype(F32)
    kv[0:B, :] = new_kv[:, :DH]
    kv[B:2 * B, :] = new_kv[:, DH:]
    for j in range(NQ):
        cols = pl.ds(j * QB, QB)
        q = jnp.dot(h[...], w[:, cols], preferred_element_type=F32) + bq_ref[:, cols]
        q = q.astype(BF16).astype(F32)
        if j < NQ - 1:
            load_wq[j + 1].wait()
        for n in range(QB // DH):
            q2[c, pl.ds(j * (QB // DH) + n, B, stride=HC), :] = q[:, n * DH:(n + 1) * DH]
    load_wo = []
    for e in range(2):
        cols = pl.ds(pl.multiple_of(c * DC + e * DY, DY), DY)
        load_wo.append(pltpu.make_async_copy(wo_hbm.at[:, cols], w.at[pl.ds(e * H * DH, H * DH)], wsem.at[NQ + e]))
        load_wo[-1].start()
    fetch(2)
    fetch(3)
    pl.semaphore_wait(bar, 3)

    def send(src, dst, ssem, rsem, dev):
        cp = pltpu.make_async_remote_copy(src, dst, ssem, rsem, device_id=dev, device_id_type=MESH)
        cp.start()
        return cp

    W = S * H
    Q = AB * HC
    swap = [send(q2.at[c, pl.ds(k * Q, Q)], q2.at[c, pl.ds(k * Q, Q)], qs.at[k], qr.at[k], mate) for k in range(B // AB)]
    hop0, hop1, hop2, hopb, hopc, hopd = {}, {}, {}, {}, {}, {}
    stages = attention_stages(lens, sq * T, q2, held, kv, o_ref, lse_ref, (b0, b1, b2, b3, b4, b5, b6, b7))
    ready = []
    lane8 = lax.broadcasted_iota(jnp.int32, (H // 2, DH), 1)

    def attend(k):
        block = k * CS // AB
        swap[block].wait_recv()
        for cp in loads[block]:
            cp.wait()
        stages(block)

    def rows_of_o(k, xx, cc):
        return pl.ds(pl.multiple_of((k * 4 + xx * 2 + cc) * W, W), W)

    def share(k):
        hop0[k] = [send(o_ref.at[rows_of_o(k, xx, 1 - c)], o_core.at[k, xx], a0s.at[k, xx], a0r.at[k, xx], mate) for xx in range(2)]
        hop0[k].append(send(lse_ref.at[pl.ds(k * H, H)], l_core.at[k], a0s.at[k, 2], a0r.at[k, 2], mate))

    def mix(k):
        for cp in hop0[k]:
            cp.wait_recv()
        shift = lax.rem(DH - c * S, DH)
        fa, fb, lm = merge(pltpu.roll(lse_ref[pl.ds(k * H, H), :], shift, 1), pltpu.roll(l_core[k], shift, 1))
        l_mix[k] = lm
        theirs = pltpu.roll(lm, lax.rem(DH - (1 - x) * R, DH), 1)
        l_half[k] = jnp.where(lane8 < S, theirs[:H // 2], pltpu.roll(theirs[H // 2:], S, 1))
        for xx in range(2):
            mine = (k * 4 + xx * 2 + c) * W
            for j in range(S):
                oa = o_ref[pl.ds(pl.multiple_of(mine + j * H, H), H), :]
                ob = o_core[k, xx, j * H:(j + 1) * H, :]
                at = xx * R + j
                o_mix[k, xx, j * H:(j + 1) * H, :] = column(fa, at) * oa + column(fb, at) * ob
        hop1[k] = [send(o_mix.at[k, 1 - x], o_x.at[k], a1s.at[k, 0], a1r.at[k, 0], over_x),
                   send(l_half.at[k], l_x.at[k], a1s.at[k, 1], a1r.at[k, 1], over_x)]

    def quarter(k):
        for cp in hop1[k]:
            cp.wait_recv()
        shift = lax.rem(DH - x * R, DH)
        l_far = jnp.concatenate([l_x[k], pltpu.roll(l_x[k], DH - S, 1)], 0)
        fa, fb, _ = merge(pltpu.roll(l_mix[k], shift, 1), l_far)
        for j in range(S):
            oa = o_mix[k, x, j * H:(j + 1) * H, :]
            ob = o_x[k, j * H:(j + 1) * H, :]
            a_all[k, pl.ds(pl.multiple_of(c * W + j * H, H), H), :] = column(fa, j) * oa + column(fb, j) * ob
        own = pl.ds(pl.multiple_of(c * W, W), W)
        hop2[k] = send(a_all.at[k, own], a_all.at[k, own], a2s.at[k], a2r.at[k], mate)

    def project(k):
        hop2[k].wait_recv()
        a = jnp.concatenate([a_all[k, pl.ds(n, R, stride=H), :].astype(BF16) for n in range(H)], 1)
        if not ready:
            for cp in load_wo:
                cp.wait()
            ready.append(1)
        for e in range(2):
            part[k, :, e * DY:(e + 1) * DY] = jnp.dot(a, w[e * H * DH:(e + 1) * H * DH, :], preferred_element_type=F32)
        hopb[k] = send(part.at[k, :, pl.ds(pl.multiple_of((1 - tp) * DY, DY), DY)], p_y.at[k], bs.at[k], br.at[k], over_y)

    def piece(k, xx, yy, lo=0, width=DY):
        return (pl.ds(pl.multiple_of(k * CS + xx * R, R), R), pl.ds(pl.multiple_of(c * DC + yy * DY + lo, 128), width))

    def pass_on(at, ssem, rsem, dev):
        return send(y_ref.at[at], y_ref.at[at], ssem, rsem, dev)

    def finish(k):
        hopb[k].wait_recv()
        at = piece(k, x, tp)
        y_ref[at] = part[k, :, pl.ds(pl.multiple_of(tp * DY, DY), DY)] + p_y[k]
        hopc[k] = [pass_on(at, cs.at[k, 0], cr.at[k, 0], over_x), pass_on(at, cs.at[k, 1], cr.at[k, 1], over_y)]
        hopd[k] = [pass_on(at, ds.at[k, 0], dr.at[k, 0], mate)]

    def relay(k):
        hopc[k][1].wait_recv()
        hopc[k].append(pass_on(piece(k, x, 1 - tp, VIA_Y, DY - VIA_Y), cs.at[k, 2], cr.at[k, 2], over_x))
        hopd[k].append(pass_on(piece(k, x, 1 - tp), ds.at[k, 1], dr.at[k, 1], mate))
        hopc[k][0].wait_recv()
        hopc[k].append(pass_on(piece(k, 1 - x, tp, 0, VIA_Y), cs.at[k, 3], cr.at[k, 3], over_y))
        hopd[k].append(pass_on(piece(k, 1 - x, tp), ds.at[k, 2], dr.at[k, 2], mate))

    def last(k):
        hopc[k][2].wait_recv()
        hopc[k][3].wait_recv()
        hopd[k].append(pass_on(piece(k, 1 - x, 1 - tp), ds.at[k, 3], dr.at[k, 3], mate))

    for step, k in SCHEDULE:
        {"a": attend, "s": share, "m": mix, "q": quarter, "p": project, "f": finish, "r": relay, "l": last}[step](k)
    for k in range(NC):
        for cp in hopd[k]:
            cp.wait_recv()
    for cp in swap:
        cp.wait_send()
    for k in range(NC):
        for cp in [*hop0[k], *hop1[k], hop2[k], hopb[k], *hopc[k], *hopd[k]]:
            cp.wait_send()


def last_kernel(lens_hbm, kv, y_in, hid_hbm, bo_hbm, held_in, ko_hbm, vo_hbm, out_hbm, held, lens, hid, bo_ref, out, sem, isem, osem):
    load = [pltpu.make_async_copy(src, dst, isem.at[e]) for e, (src, dst) in enumerate(((lens_hbm, lens), (bo_hbm, bo_ref), (hid_hbm, hid)))]
    for cp in load:
        cp.start()

    def rows(i, _):
        r = pl.ds(pl.multiple_of(i * 16, 16), 16)
        out[r, :] = (hid[r, :].astype(F32) + y_in[r, :] + bo_ref[...]).astype(BF16)
        return 0

    first = lax.axis_index("sq") * T
    copies = []

    def put(k):
        insert_rows(lens, first, kv, held, k * AB, (k + 1) * AB)
        for e, dst in enumerate((ko_hbm, vo_hbm)):
            copies.append(pltpu.make_async_copy(held.at[pl.ds(e * B + k * AB, AB)], dst.at[pl.ds(k * AB, AB)], sem.at[2 * k + e]))
            copies[-1].start()

    load[0].wait()
    put(0)
    load[1].wait()
    load[2].wait()
    lax.fori_loop(0, B // 16, rows, 0, unroll=2)
    copies.append(pltpu.make_async_copy(out, out_hbm, osem))
    copies[-1].start()
    for k in range(1, B // AB):
        put(k)
    for cp in copies:
        cp.wait()


def solution(mesh):
    def local_step(hidden, cache_lens, k_cache, v_cache, ln_gain, ln_bias, w_query, b_query, w_kv, b_kv, w_out, b_out):
        hbm = pl.BlockSpec(memory_space=pltpu.HBM)
        vm = pl.BlockSpec(memory_space=pltpu.VMEM)
        sem = pltpu.SemaphoreType.DMA

        def pin(*arrays):
            return [pltpu.with_memory_space_constraint(a, pltpu.VMEM) for a in arrays]

        def far(*arrays):
            return [pltpu.with_memory_space_constraint(a, pltpu.HBM) for a in arrays]

        held = pltpu.VMEM((2 * B, T, DH), BF16)
        y, kv_held, kv = pl.pallas_call(
            step_kernel,
            out_shape=(pltpu.VMEM((B, D), F32), held, pltpu.VMEM((2 * B, DH), F32)),
            in_specs=[hbm] * 11,
            out_specs=(vm, vm, vm),
            scratch_shapes=[
                pltpu.SMEM((B,), jnp.int32), pltpu.VMEM((1, D), F32), pltpu.VMEM((1, D), F32), pltpu.VMEM((1, HC * DH), F32), pltpu.VMEM((1, 2 * DH), F32),
                pltpu.VMEM((B, D), BF16), pltpu.VMEM((D, HC * DH), BF16), pltpu.VMEM((D, 2 * DH), BF16), pltpu.VMEM((2, B * HC, DH), F32),
                pltpu.VMEM((B * H, DH), F32), pltpu.VMEM((NC * H, DH), F32), *STAGE_BUFS,
                pltpu.VMEM((NC, 2, S * H, DH), F32), pltpu.VMEM((NC, H, DH), F32),
                pltpu.VMEM((NC, 2, S * H, DH), F32), pltpu.VMEM((NC, H, DH), F32), pltpu.VMEM((NC, H // 2, DH), F32),
                pltpu.VMEM((NC, S * H, DH), F32), pltpu.VMEM((NC, H // 2, DH), F32),
                pltpu.VMEM((NC, R * H, DH), F32), pltpu.VMEM((NC, R, DC), F32), pltpu.VMEM((NC, R, DY), F32),
                sem((3,)), sem((5,)), sem((NQ + 2,)), sem((2 * (B // AB),)), sem((B // AB,)), sem((B // AB,)),
                sem((NC, 3)), sem((NC, 3)), sem((NC, 2)), sem((NC, 2)), sem((NC,)), sem((NC,)),
                sem((NC,)), sem((NC,)), sem((NC, 4)), sem((NC, 4)), sem((NC, 4)), sem((NC, 4)),
            ],
            compiler_params=pltpu.CompilerParams(vmem_limit_bytes=MLIM, collective_id=0, has_side_effects=True),
            name="step",
        )(*far(cache_lens, hidden, k_cache, v_cache, ln_gain[None], ln_bias[None], w_query, b_query[None], w_kv, b_kv[None], w_out))
        cache = jax.ShapeDtypeStruct((B, T, DH), BF16)
        k_new, v_new, out_hidden, _ = pl.pallas_call(
            last_kernel,
            out_shape=(cache, cache, jax.ShapeDtypeStruct((B, D), BF16), held),
            in_specs=[hbm, vm, vm, hbm, hbm, vm],
            out_specs=(hbm, hbm, hbm, vm),
            input_output_aliases={5: 3},
            scratch_shapes=[pltpu.SMEM((B,), jnp.int32), pltpu.VMEM((B, D), BF16), pltpu.VMEM((1, D), F32), pltpu.VMEM((B, D), BF16),
                            sem((2 * (B // AB),)), sem((3,)), sem],
            compiler_params=pltpu.CompilerParams(vmem_limit_bytes=24 * MIB),
            name="last",
        )(*far(cache_lens), *pin(kv, y), *far(hidden, b_out[None]), *pin(kv_held))
        return out_hidden, k_new, v_new

    cache_spec = P("dp", "sq", None)
    row_spec = P("dp", None)
    in_specs = (row_spec, P("dp"), cache_spec, cache_spec, P(None), P(None), P(None, "tp"), P("tp"), P(None, None), P(None), P("tp", None), P(None))
    out_specs = (row_spec, cache_spec, cache_spec)
    return jax.shard_map(local_step, mesh=mesh, in_specs=in_specs, out_specs=out_specs, check_vma=False)
```

time: 74 us -> 74.5 us (level)
    pallas_call x1, Pallas kernels: 10.4 us -> 13 us  [local_step(): pl.pallas_call(last_kernel, out_shape=(cache, cache, jax.ShapeDtypeStruct...]
    pallas_call x2 -> x1, Pallas kernels: 62.6 us -> 60.6 us  [local_step(): pl.pallas_call(step_kernel, out_shape=(pltpu.VMEM((B, D), F32), held, plt...]
where the time goes in v6:
time: 74.5 us; the launch traced here: 74.3 us
  Pallas kernels  73.5 us (99%)
  between operations  0.8 us (1%)
    pallas_call x1, Pallas kernels, local_step(): pl.pallas_call(step_kernel, out_shape=(pltpu.VMEM((B, D), F32), held, plt...  60.6 us
    pallas_call x1, Pallas kernels, local_step(): pl.pallas_call(last_kernel, out_shape=(cache, cache, jax.ShapeDtypeStruct...  13 us

profile of v6, /device:TPU:0, one launch (start us, length us, event | category | flops | bytes accessed | tf_op | source)
XLA Modules:
  0.0 74.3 jit_solution(12079187175549385330)
XLA Ops:
  0.6 60.6 %step.1 = (f32[256,4096]{1,0:T(8,128)S(1)}, bf16[512,256,128]{2,1,0:T(8,128)(2,1)S(1)}, f32[512,128]{1,0:T(8,128)S(1)}) custom-call(s32[256]{0:T(256)} %lens_hbm.3, bf16[256,4096]{1,0:T(8,128)(2,1)} %hid_hbm.3, bf16[256,256,128]{2,1,0:T(8,128)(2,1)} %k_hbm.1, bf16[256,256,128]{2,1,0:T(8,128)(2,1)} %v_hbm.1, f32[1,4096]{1,0:T(1,128)} %bitcast.5, ...), custom_call_target="tpu_custom_call" | custom-call | tf_op jit(solution)/shard_map/step/pallas_call | solution.py:372
  61.2 13.0 %last.1 = (bf16[256,256,128]{2,1,0:T(8,128)(2,1)}, bf16[256,256,128]{2,1,0:T(8,128)(2,1)}, bf16[256,4096]{1,0:T(8,128)(2,1)}, bf16[512,256,128]{2,1,0:T(8,128)(2,1)S(1)}) custom-call(s32[256]{0:T(256)} %lens_hbm.3, f32[512,128]{1,0:T(8,128)S(1)} %get-tuple-element.9.kv, f32[256,4096]{1,0:T(8,128)S(1)} %get-tuple-element.10.y_in, ...), custom_call_target="tpu_custom_call", output_to_operand_aliasing={{3}: (5, {})} | custom-call | tf_op jit(solution)/shard_map/last/pallas_call | solution.py:393

commit v7 on v6

--- a/solution.py
+++ b/solution.py
@@ -31,9 +31,9 @@
 GROUP = 8
 MIB = 1024 * 1024
 MLIM = 24 * MIB
-VIA_Y = 256
+VIA_Y = 384
 SCHEDULE = [(s[0], int(s[1])) for s in (
-    "a0", "s0", "s1", "a2", "m0", "s2", "m1", "a4", "m2", "q0", "s5", "a6", "m5", "s3", "q1", "s7", "s4", "p0", "q2", "s6", "m3", "p1", "m4", "p2", "m6", "q5", "f0", "q3", "m7", "q4", "f1", "p3", "p4", "q6", "r0", "p5", "q7", "f2", "p6", "r1", "p7", "f4", "f3", "f5", "l0", "f6", "f7", "r2", "r3", "r4", "r5", "r6", "r7", "l1", "l2", "l3", "l4", "l5", "l6", "l7")]
+    "a0", "s0", "s1", "a2", "s3", "s2", "m1", "m0", "a4", "m2", "s4", "a6", "s5", "q0", "m4", "s6", "q1", "m3", "s7", "q2", "p0", "p1", "p2", "m5", "q3", "m6", "f0", "m7", "f1", "q4", "p3", "q5", "f2", "p4", "q6", "p5", "f3", "q7", "p6", "r1", "p7", "f5", "f4", "f6", "r0", "l1", "f7", "r5", "r3", "r4", "r2", "r6", "r7", "l5", "l4", "l3", "l0", "l2", "l6", "l7")]
 def attention_stages(lens, first, q2, held, kv, o_ref, lse_ref, bufs):
     lane = lax.broadcasted_iota(jnp.int32, (H, DH), 1)
     pos = lax.broadcasted_iota(jnp.int32, (H, T), 1)
@@ -96,7 +96,7 @@
         score(lo + 1, s_b)
         soften(lo, s_a, p_a, r_a, n_a)
 
-        def body(t, _):
+        def body(t):
             i = lo + 2 + 2 * t
             score(i, s_a)
             soften(i - 1, s_b, p_b, r_b, n_b)
@@ -104,9 +104,9 @@
             score(i + 1, s_b)
             soften(i, s_a, p_a, r_a, n_a)
             weigh(i - 1, p_b, r_b, n_b)
-            return 0
-
-        lax.fori_loop(0, (hi - lo - 2) // 2, body, 0)
+
+        for t in range((hi - lo - 2) // 2):
+            body(t)
         soften(hi - 1, s_b, p_b, r_b, n_b)
         weigh(hi - 2, p_a, r_a, n_a)
         weigh(hi - 1, p_b, r_b, n_b)
@@ -146,7 +146,7 @@
 
 def step_kernel(lens_hbm, hid_hbm, k_hbm, v_hbm, gain_hbm, bias_hbm, wq_hbm, bq_hbm, wkv_hbm, bkv_hbm, wo_hbm,
                 y_ref, held, kv,
-                lens, gain_ref, bias_ref, bq_ref, bkv_ref, h, w, wkv, q2, o_ref, lse_ref, b0, b1, b2, b3, b4, b5, b6, b7,
+                lens, gain_ref, bias_ref, bq_ref, bkv_ref, h, mean_ref, rstd_ref, w, wkv, q2, o_ref, lse_ref, b0, b1, b2, b3, b4, b5, b6, b7,
                 o_core, l_core, o_mix, l_mix, l_half, o_x, l_x, a_all, part, p_y,
                 hsem, ssem, wsem, csem, qs, qr, a0s, a0r, a1s, a1r, a2s, a2r, bs, br, cs, cr, ds, dr):
     sq, tp = lax.axis_index("sq"), lax.axis_index("tp")
@@ -181,18 +181,34 @@
     small[0].wait()
     small[1].wait()
 
-    def norm_rows(i, _):
-        rows = pl.ds(pl.multiple_of(i * 16, 16), 16)
-        wide = h[rows, :].astype(F32)
-        mean = jnp.sum(wide, axis=-1, keepdims=True) * (1.0 / D)
-        cen = wide - mean
+    def spread(tile):
+        return jnp.concatenate([tile] * (D // DH), 1)
+
+    def block(i):
+        return pl.ds(pl.multiple_of(i * 16, 16), 16)
+
+    def means(i, _):
+        total = jnp.sum(h[block(i), :].astype(F32), axis=-1, keepdims=True)
+        mean_ref[block(i), :] = jnp.broadcast_to(total * (1.0 / D), (16, DH))
+        return 0
+
+    def scales(i, _):
+        cen = h[block(i), :].astype(F32) - spread(mean_ref[block(i), :])
         var = jnp.sum(cen * cen, axis=-1, keepdims=True) * (1.0 / D)
-        h[rows, :] = (cen * lax.rsqrt(var + 1e-5) * gain_ref[...] + bias_ref[...]).astype(BF16)
+        rstd_ref[block(i), :] = jnp.broadcast_to(lax.rsqrt(var + 1e-5), (16, DH))
+        return 0
+
+    def normed(i, _):
+        y = (h[block(i), :].astype(F32) - spread(mean_ref[block(i), :])) * spread(rstd_ref[block(i), :])
+        h[block(i), :] = (y * gain_ref[...] + bias_ref[...]).astype(BF16)
         return 0
 
     for e in range(2):
         load_h[e].wait()
-        lax.fori_loop(e * (B // 32), (e + 1) * (B // 32), norm_rows, 0, unroll=2)
+        lo, hi = e * (B // 32), (e + 1) * (B // 32)
+        lax.fori_loop(lo, hi, means, 0, unroll=4)
+        lax.fori_loop(lo, hi, scales, 0, unroll=4)
+        lax.fori_loop(lo, hi, normed, 0, unroll=2)
     load_wkv.wait()
     for cp in small[2:]:
         cp.wait()
@@ -337,21 +353,25 @@
     first = lax.axis_index("sq") * T
     copies = []
 
-    def put(k):
-        insert_rows(lens, first, kv, held, k * AB, (k + 1) * AB)
+    def put(lo, hi):
+        insert_rows(lens, first, kv, held, lo, hi)
         for e, dst in enumerate((ko_hbm, vo_hbm)):
-            copies.append(pltpu.make_async_copy(held.at[pl.ds(e * B + k * AB, AB)], dst.at[pl.ds(k * AB, AB)], sem.at[2 * k + e]))
+            copies.append(pltpu.make_async_copy(held.at[pl.ds(e * B + lo, hi - lo)], dst.at[pl.ds(lo, hi - lo)], sem.at[len(copies)]))
             copies[-1].start()
 
     load[0].wait()
-    put(0)
+    put(0, 16)
+    put(16, 32)
+    put(32, 64)
+    put(64, 128)
     load[1].wait()
     load[2].wait()
     lax.fori_loop(0, B // 16, rows, 0, unroll=2)
-    copies.append(pltpu.make_async_copy(out, out_hbm, osem))
-    copies[-1].start()
-    for k in range(1, B // AB):
-        put(k)
+    store_out = pltpu.make_async_copy(out, out_hbm, osem)
+    store_out.start()
+    put(128, 192)
+    put(192, 256)
+    store_out.wait()
     for cp in copies:
         cp.wait()
 
@@ -376,7 +396,7 @@
             out_specs=(vm, vm, vm),
             scratch_shapes=[
                 pltpu.SMEM((B,), jnp.int32), pltpu.VMEM((1, D), F32), pltpu.VMEM((1, D), F32), pltpu.VMEM((1, HC * DH), F32), pltpu.VMEM((1, 2 * DH), F32),
-                pltpu.VMEM((B, D), BF16), pltpu.VMEM((D, HC * DH), BF16), pltpu.VMEM((D, 2 * DH), BF16), pltpu.VMEM((2, B * HC, DH), F32),
+                pltpu.VMEM((B, D), BF16), pltpu.VMEM((B, DH), F32), pltpu.VMEM((B, DH), F32), pltpu.VMEM((D, HC * DH), BF16), pltpu.VMEM((D, 2 * DH), BF16), pltpu.VMEM((2, B * HC, DH), F32),
                 pltpu.VMEM((B * H, DH), F32), pltpu.VMEM((NC * H, DH), F32), *STAGE_BUFS,
                 pltpu.VMEM((NC, 2, S * H, DH), F32), pltpu.VMEM((NC, H, DH), F32),
                 pltpu.VMEM((NC, 2, S * H, DH), F32), pltpu.VMEM((NC, H, DH), F32), pltpu.VMEM((NC, H // 2, DH), F32),
@@ -397,7 +417,7 @@
             out_specs=(hbm, hbm, hbm, vm),
             input_output_aliases={5: 3},
             scratch_shapes=[pltpu.SMEM((B,), jnp.int32), pltpu.VMEM((B, D), BF16), pltpu.VMEM((1, D), F32), pltpu.VMEM((B, D), BF16),
-                            sem((2 * (B // AB),)), sem((3,)), sem],
+                            sem((12,)), sem((3,)), sem],
             compiler_params=pltpu.CompilerParams(vmem_limit_bytes=24 * MIB),
             name="last",
         )(*far(cache_lens), *pin(kv, y), *far(hidden, b_out[None]), *pin(kv_held))

time: 74.5 us -> 73.4 us (0.985)
  Pallas kernels: 73.5 us -> 72.4 us
where the time goes in v7:
time: 73.4 us; the launch traced here: 73.2 us
  Pallas kernels  72.4 us (99%)
  between operations  0.8 us (1%)
    pallas_call x1, Pallas kernels, local_step(): pl.pallas_call(step_kernel, out_shape=(pltpu.VMEM((B, D), F32), held, plt...  59.8 us
    pallas_call x1, Pallas kernels, local_step(): pl.pallas_call(last_kernel, out_shape=(cache, cache, jax.ShapeDtypeStruct...  12.6 us

profile of v7, /device:TPU:0, one launch (start us, length us, event | category | flops | bytes accessed | tf_op | source)
XLA Modules:
  0.0 73.2 jit_solution(8816812573775996230)
XLA Ops:
  0.6 59.8 %step.1 = (f32[256,4096]{1,0:T(8,128)S(1)}, bf16[512,256,128]{2,1,0:T(8,128)(2,1)S(1)}, f32[512,128]{1,0:T(8,128)S(1)}) custom-call(s32[256]{0:T(256)} %lens_hbm.3, bf16[256,4096]{1,0:T(8,128)(2,1)} %hid_hbm.3, bf16[256,256,128]{2,1,0:T(8,128)(2,1)} %k_hbm.1, bf16[256,256,128]{2,1,0:T(8,128)(2,1)} %v_hbm.1, f32[1,4096]{1,0:T(1,128)} %bitcast.5, ...), custom_call_target="tpu_custom_call" | custom-call | tf_op jit(solution)/shard_map/step/pallas_call | solution.py:392
  60.5 12.6 %last.1 = (bf16[256,256,128]{2,1,0:T(8,128)(2,1)}, bf16[256,256,128]{2,1,0:T(8,128)(2,1)}, bf16[256,4096]{1,0:T(8,128)(2,1)}, bf16[512,256,128]{2,1,0:T(8,128)(2,1)S(1)}) custom-call(s32[256]{0:T(256)} %lens_hbm.3, f32[512,128]{1,0:T(8,128)S(1)} %get-tuple-element.9.kv, f32[256,4096]{1,0:T(8,128)S(1)} %get-tuple-element.10.y_in, ...), custom_call_target="tpu_custom_call", output_to_operand_aliasing={{3}: (5, {})} | custom-call | tf_op jit(solution)/shard_map/last/pallas_call | solution.py:413

commit v8 on v5

--- a/solution.py
+++ b/solution.py
@@ -30,7 +30,9 @@
 GROUP = 8
 MIB = 1024 * 1024
 VIA_Y = 128
-SCHEDULE = [(s[0], int(s[1])) for s in "s0 s1 m0 a2 m1 s2 s3 a4 s4 s5 m2 m3 q0 m4 q1 m5 p0 p1 q2 a6 f0 q3 s6 s7 q4 f1 p2 m6 m7 p3 r0 p4 f2 q5 q6 q7 f3 r1 p5 f4 r2 p6 l0 l1 r3 p7 f5 r4 f6 f7 l2 r5 l3 l4 r6 r7 l5 l6 l7".split()]
+SCHEDULE = [(s[0], int(s[1])) for s in (
+    "s0", "s1", "m0", "a2", "m1", "s2", "s3", "a4", "s4", "s5", "m2", "m3", "q0", "m4", "q1", "m5", "p0", "p1", "q2", "a6", "f0", "q3", "s6", "s7", "q4", "f1", "p2", "m6", "m7", "p3", "r0", "p4", "f2", "q5", "q6", "q7", "f3", "r1", "p5", "f4", "r2", "p6", "l0", "l1", "r3", "p7", "f5", "r4", "f6", "f7", "l2", "r5", "l3", "l4", "r6", "r7", "l5", "l6", "l7")]
+
 def attention_stages(lens, first, q3, kbuf, vbuf, base, vbase, kv, o_ref, lse_ref, bufs):
     lane = lax.broadcasted_iota(jnp.int32, (H, DH), 1)
     pos = lax.broadcasted_iota(jnp.int32, (H, T), 1)
@@ -89,7 +91,7 @@
         score(lo + 1, s_b)
         soften(lo, s_a, p_a, r_a, n_a)
 
-        def body(t, _):
+        def body(t):
             i = lo + 2 + 2 * t
             score(i, s_a)
             soften(i - 1, s_b, p_b, r_b, n_b)
@@ -97,9 +99,9 @@
             score(i + 1, s_b)
             soften(i, s_a, p_a, r_a, n_a)
             weigh(i - 1, p_b, r_b, n_b)
-            return 0
-
-        lax.fori_loop(0, (hi - lo - 2) // 2, body, 0)
+
+        for t in range((hi - lo - 2) // 2):
+            body(t)
         soften(hi - 1, s_b, p_b, r_b, n_b)
         weigh(hi - 2, p_a, r_a, n_a)
         weigh(hi - 1, p_b, r_b, n_b)
@@ -128,14 +130,14 @@
 
 def first_kernel(lens_hbm, hid_hbm, k_hbm, v_hbm, gain_hbm, bias_hbm, wq_hbm, bq_hbm, wkv_hbm, bkv_hbm,
                  q3, kv, o_ref, lse_ref, ko_hbm, vo_hbm,
-                 lens, gain_ref, bias_ref, bq_ref, bkv_ref, hid, h, wq, wkv, kbuf, vbuf, b0, b1, b2, b3, b4, b5, b6, b7, wsem, csem, ssem):
+                 lens, gain_ref, bias_ref, bq_ref, bkv_ref, h, mean_ref, rstd_ref, wq, wkv, kbuf, vbuf, b0, b1, b2, b3, b4, b5, b6, b7, wsem, csem, ssem):
     first = lax.axis_index("sq") * T
     small = [pltpu.make_async_copy(src, dst, ssem.at[e]) for e, (src, dst) in enumerate((
         (gain_hbm, gain_ref), (bias_hbm, bias_ref), (bkv_hbm, bkv_ref), (bq_hbm, bq_ref), (lens_hbm, lens)))]
     load_h = []
     for e in range(2):
         rows = pl.ds(e * (B // 2), B // 2)
-        load_h.append(pltpu.make_async_copy(hid_hbm.at[rows], hid.at[rows], wsem.at[NQ + e]))
+        load_h.append(pltpu.make_async_copy(hid_hbm.at[rows], h.at[rows], wsem.at[NQ + e]))
         load_h[-1].start()
         if e == 0:
             for cp in small:
@@ -152,19 +154,34 @@
     small[0].wait()
     small[1].wait()
 
-    def norm_rows(i, _):
-        rows = pl.ds(pl.multiple_of(i * 16, 16), 16)
-        x = hid[rows, :].astype(F32)
-        mean = jnp.sum(x, axis=-1, keepdims=True) * (1.0 / D)
-        cen = x - mean
+    def spread(tile):
+        return jnp.concatenate([tile] * (D // DH), 1)
+
+    def block(i):
+        return pl.ds(pl.multiple_of(i * 16, 16), 16)
+
+    def means(i, _):
+        total = jnp.sum(h[block(i), :].astype(F32), axis=-1, keepdims=True)
+        mean_ref[block(i), :] = jnp.broadcast_to(total * (1.0 / D), (16, DH))
+        return 0
+
+    def scales(i, _):
+        cen = h[block(i), :].astype(F32) - spread(mean_ref[block(i), :])
         var = jnp.sum(cen * cen, axis=-1, keepdims=True) * (1.0 / D)
-        y = cen * lax.rsqrt(var + 1e-5)
-        h[rows, :] = (y * gain_ref[...] + bias_ref[...]).astype(BF16)
+        rstd_ref[block(i), :] = jnp.broadcast_to(lax.rsqrt(var + 1e-5), (16, DH))
+        return 0
+
+    def normed(i, _):
+        y = (h[block(i), :].astype(F32) - spread(mean_ref[block(i), :])) * spread(rstd_ref[block(i), :])
+        h[block(i), :] = (y * gain_ref[...] + bias_ref[...]).astype(BF16)
         return 0
 
     for e in range(2):
         load_h[e].wait()
-        lax.fori_loop(e * (B // 32), (e + 1) * (B // 32), norm_rows, 0, unroll=2)
+        lo, hi = e * (B // 32), (e + 1) * (B // 32)
+        lax.fori_loop(lo, hi, means, 0, unroll=4)
+        lax.fori_loop(lo, hi, scales, 0, unroll=4)
+        lax.fori_loop(lo, hi, normed, 0, unroll=2)
     load_wkv.wait()
     for cp in small[2:]:
         cp.wait()
@@ -354,18 +371,21 @@
     n = B - AB
     copies = []
 
-    def put(k):
-        insert_rows(lens, first, kv, (held.at[pl.ds(0, n)], held.at[pl.ds(n, n)]), k * AB, (k + 1) * AB, AB)
+    def put(lo, hi):
+        insert_rows(lens, first, kv, (held.at[pl.ds(0, n)], held.at[pl.ds(n, n)]), lo, hi, AB)
         for e, dst in enumerate((ko_hbm, vo_hbm)):
-            copies.append(pltpu.make_async_copy(held.at[pl.ds(e * n + (k - 1) * AB, AB)], dst.at[pl.ds(k * AB, AB)], sem.at[2 * k + e - 2]))
+            copies.append(pltpu.make_async_copy(held.at[pl.ds(e * n + lo - AB, hi - lo)], dst.at[pl.ds(lo, hi - lo)], sem.at[len(copies)]))
             copies[-1].start()
 
-    put(1)
+    put(64, 80)
+    put(80, 96)
+    put(96, 128)
     lax.fori_loop(B // 32, B // 16, rows, 0, unroll=2)
-    copies.append(pltpu.make_async_copy(out, out_hbm, osem))
-    copies[-1].start()
-    for k in range(2, B // AB):
-        put(k)
+    store_out = pltpu.make_async_copy(out, out_hbm, osem)
+    store_out.start()
+    put(128, 192)
+    put(192, 256)
+    store_out.wait()
     for cp in copies:
         cp.wait()
 
@@ -391,7 +411,7 @@
             out_specs=(vm, vm, vm, vm, hbm, hbm),
             scratch_shapes=[
                 pltpu.SMEM((B,), jnp.int32), pltpu.VMEM((1, D), F32), pltpu.VMEM((1, D), F32), pltpu.VMEM((1, H * DH), F32), pltpu.VMEM((1, 2 * DH), F32),
-                pltpu.VMEM((B, D), BF16), pltpu.VMEM((B, D), BF16), pltpu.VMEM((D, H * DH), BF16), pltpu.VMEM((D, 2 * DH), BF16),
+                pltpu.VMEM((B, D), BF16), pltpu.VMEM((B, DH), F32), pltpu.VMEM((B, DH), F32), pltpu.VMEM((D, H * DH), BF16), pltpu.VMEM((D, 2 * DH), BF16),
                 pltpu.VMEM((AB, T, DH), BF16), pltpu.VMEM((AB, T, DH), BF16), *STAGE_BUFS, sem((NQ + 3,)), sem((4,)), sem((5,)),
             ],
             compiler_params=pltpu.CompilerParams(vmem_limit_bytes=33 * MIB),
@@ -422,7 +442,7 @@
             in_specs=[hbm, vm, vm, vm, vm, vm, hbm, hbm],
             out_specs=(hbm, hbm, hbm, vm),
             input_output_aliases={5: 3, 6: 0, 7: 1},
-            scratch_shapes=[pltpu.SMEM((B,), jnp.int32), pltpu.VMEM((B, D), BF16), sem((2 * (B // AB) - 2,)), sem],
+            scratch_shapes=[pltpu.SMEM((B,), jnp.int32), pltpu.VMEM((B, D), BF16), sem((10,)), sem],
             compiler_params=pltpu.CompilerParams(vmem_limit_bytes=6 * MIB),
             name="last",
         )(*far(cache_lens), *pin(kv, y), hidden, b_out[None], *pin(kv_held), k_part, v_part)

time: 74 us -> 72.4 us (0.978)
  Pallas kernels: 73 us -> 71.4 us
    pallas_call x1, Pallas kernels: 48.1 us -> 46.7 us  [local_step(): pl.pallas_call(exchange_kernel, out_shape=(pltpu.VMEM((B, D), F32), held)...]
where the time goes in v8:
time: 72.4 us; the launch traced here: 72.3 us
  Pallas kernels  71.4 us (99%)
  between operations  0.86 us (1%)
    pallas_call x1, Pallas kernels, local_step(): pl.pallas_call(exchange_kernel, out_shape=(pltpu.VMEM((B, D), F32), held)...  46.7 us
    pallas_call x1, Pallas kernels, local_step(): pl.pallas_call(first_kernel, out_shape=(pltpu.VMEM((B * H, DH), F32), plt...  14.7 us
    pallas_call x1, Pallas kernels, local_step(): pl.pallas_call(last_kernel, out_shape=(cache, cache, jax.ShapeDtypeStruct...  10 us

profile of v8, /device:TPU:0, one launch (start us, length us, event | category | flops | bytes accessed | tf_op | source)
XLA Modules:
  0.0 72.3 jit_solution(14389802940076502767)
XLA Ops:
  0.6 14.7 %first.1 = (f32[4096,128]{1,0:T(8,128)S(1)}, f32[512,128]{1,0:T(8,128)S(1)}, f32[1024,128]{1,0:T(8,128)S(1)}, f32[32,128]{1,0:T(8,128)S(1)}, bf16[256,256,128]{2...) custom-call(s32[256]{0:T(256)} %lens_hbm.5, bf16[256,4096]{1,0:T(8,128)(2,1)} %hid.1, bf16[256,256,128]{2,1,0:T(8,128)(2,1)} %k_hbm.3, ...), custom_call_target="tpu_custom_call" | custom-call | tf_op jit(solution)/shard_map/first/pallas_call | solution.py:407
  15.3 0.0 copy-start
  15.3 0.0 copy-start.1
  15.4 46.7 %exchange.1 = (f32[256,4096]{1,0:T(8,128)S(1)}, bf16[384,256,128]{2,1,0:T(8,128)(2,1)S(1)}) custom-call(s32[256]{0:T(256)} %lens_hbm.5, f32[4096,128]{1,0:T(8,128)S(1)} %get-tuple-element.15.q3, f32[512,128]{1,0:T(8,128)S(1)} %get-tuple-element.14.kv, f32[1024,128]{1,0:T(8,128)S(1)} %get-tuple-element.16.o_first, f32[32,128]{1,0:T(8,128)S(1)} %get-tuple-element.17.lse_first, ...), custom_call_target="tpu_custom_call" | custom-call | tf_op jit(solution)/shard_map/exchange/pallas_call | solution.py:421
  62.1 0.0 copy-done
  62.1 0.0 copy-done.1
  62.1 10.0 %last.1 = (bf16[256,256,128]{2,1,0:T(8,128)(2,1)}, bf16[256,256,128]{2,1,0:T(8,128)(2,1)}, bf16[256,4096]{1,0:T(8,128)(2,1)}, bf16[384,256,128]{2,1,0:T(8,128)(2,1)S(1)}) custom-call(s32[256]{0:T(256)} %lens_hbm.5, f32[512,128]{1,0:T(8,128)S(1)} %get-tuple-element.14.kv, ...), custom_call_target="tpu_custom_call", output_to_operand_aliasing={{3}: (5, {}), {0}: (6, {}), {1}: (7, {})} | custom-call | tf_op jit(solution)/shard_map/last/pallas_call | solution.py:439
Async XLA Ops:
  15.3 46.8 %copy-start = (bf16[256,4096]{1,0:T(8,128)(2,1)S(1)}, bf16[256,4096]{1,0:T(8,128)(2,1)}, u32[]{:S(2)}) copy-start(bf16[256,4096]{1,0:T(8,128)(2,1)} %hid.1) | copy-start | bytes 6291460
  15.3 46.8 %copy-start.1 = (f32[4096]{0:T(1024)S(1)}, f32[4096]{0:T(1024)}, u32[]{:S(2)}) copy-start(f32[4096]{0:T(1024)} %param.23) | copy-start | bytes 49156

commit v9 on v8

--- a/solution.py
+++ b/solution.py
@@ -18,7 +18,7 @@
 DH = 128
 T = 256
 AB = 64
-NC = 8
+NC = 4
 CS = B // NC
 S = CS // 4
 R = 2 * S
@@ -29,9 +29,9 @@
 QSCALE = DH ** -0.5 * math.log2(math.e)
 GROUP = 8
 MIB = 1024 * 1024
-VIA_Y = 128
+VIA_Y = 384
 SCHEDULE = [(s[0], int(s[1])) for s in (
-    "s0", "s1", "m0", "a2", "m1", "s2", "s3", "a4", "s4", "s5", "m2", "m3", "q0", "m4", "q1", "m5", "p0", "p1", "q2", "a6", "f0", "q3", "s6", "s7", "q4", "f1", "p2", "m6", "m7", "p3", "r0", "p4", "f2", "q5", "q6", "q7", "f3", "r1", "p5", "f4", "r2", "p6", "l0", "l1", "r3", "p7", "f5", "r4", "f6", "f7", "l2", "r5", "l3", "l4", "r6", "r7", "l5", "l6", "l7")]
+    "s0", "a1", "s1", "m0", "a2", "s2", "m1", "m2", "q0", "a3", "s3", "q1", "p0", "m3", "p1", "q2", "f0", "q3", "p2", "p3", "f1", "f2", "f3", "r0", "r1", "r2", "r3", "l0", "l1", "l2", "l3")]
 
 def attention_stages(lens, first, q3, kbuf, vbuf, base, vbase, kv, o_ref, lse_ref, bufs):
     lane = lax.broadcasted_iota(jnp.int32, (H, DH), 1)

time: 72.4 us -> 74.4 us (1.028)
  Pallas kernels: 71.4 us -> 73.4 us
    pallas_call x1, Pallas kernels: 46.7 us -> 48.7 us  [local_step(): pl.pallas_call(exchange_kernel, out_shape=(pltpu.VMEM((B, D), F32), held)...]
where the time goes in v9:
time: 74.4 us; the launch traced here: 74.3 us
  Pallas kernels  73.4 us (99%)
  between operations  0.84 us (1%)
    pallas_call x1, Pallas kernels, local_step(): pl.pallas_call(exchange_kernel, out_shape=(pltpu.VMEM((B, D), F32), held)...  48.7 us
    pallas_call x1, Pallas kernels, local_step(): pl.pallas_call(first_kernel, out_shape=(pltpu.VMEM((B * H, DH), F32), plt...  14.7 us
    pallas_call x1, Pallas kernels, local_step(): pl.pallas_call(last_kernel, out_shape=(cache, cache, jax.ShapeDtypeStruct...  10 us

profile of v9, /device:TPU:0, one launch (start us, length us, event | category | flops | bytes accessed | tf_op | source)
XLA Modules:
  0.0 74.3 jit_solution(5386625909768247773)
XLA Ops:
  0.6 14.7 %first.1 = (f32[4096,128]{1,0:T(8,128)S(1)}, f32[512,128]{1,0:T(8,128)S(1)}, f32[1024,128]{1,0:T(8,128)S(1)}, f32[16,128]{1,0:T(8,128)S(1)}, bf16[256,256,128]{2...) custom-call(s32[256]{0:T(256)} %lens_hbm.5, bf16[256,4096]{1,0:T(8,128)(2,1)} %hid.1, bf16[256,256,128]{2,1,0:T(8,128)(2,1)} %k_hbm.3, ...), custom_call_target="tpu_custom_call" | custom-call | tf_op jit(solution)/shard_map/first/pallas_call | solution.py:407
  15.3 0.0 copy-start
  15.3 0.0 copy-start.1
  15.4 48.7 %exchange.1 = (f32[256,4096]{1,0:T(8,128)S(1)}, bf16[384,256,128]{2,1,0:T(8,128)(2,1)S(1)}) custom-call(s32[256]{0:T(256)} %lens_hbm.5, f32[4096,128]{1,0:T(8,128)S(1)} %get-tuple-element.15.q3, f32[512,128]{1,0:T(8,128)S(1)} %get-tuple-element.14.kv, f32[1024,128]{1,0:T(8,128)S(1)} %get-tuple-element.16.o_first, f32[16,128]{1,0:T(8,128)S(1)} %get-tuple-element.17.lse_first, ...), custom_call_target="tpu_custom_call" | custom-call | tf_op jit(solution)/shard_map/exchange/pallas_call | solution.py:421
  64.1 0.0 copy-done
  64.1 0.0 copy-done.1
  64.1 10.0 %last.1 = (bf16[256,256,128]{2,1,0:T(8,128)(2,1)}, bf16[256,256,128]{2,1,0:T(8,128)(2,1)}, bf16[256,4096]{1,0:T(8,128)(2,1)}, bf16[384,256,128]{2,1,0:T(8,128)(2,1)S(1)}) custom-call(s32[256]{0:T(256)} %lens_hbm.5, f32[512,128]{1,0:T(8,128)S(1)} %get-tuple-element.14.kv, ...), custom_call_target="tpu_custom_call", output_to_operand_aliasing={{3}: (5, {}), {0}: (6, {}), {1}: (7, {})} | custom-call | tf_op jit(solution)/shard_map/last/pallas_call | solution.py:439
Async XLA Ops:
  15.3 48.8 %copy-start = (bf16[256,4096]{1,0:T(8,128)(2,1)S(1)}, bf16[256,4096]{1,0:T(8,128)(2,1)}, u32[]{:S(2)}) copy-start(bf16[256,4096]{1,0:T(8,128)(2,1)} %hid.1) | copy-start | bytes 6291460
  15.3 48.8 %copy-start.1 = (f32[4096]{0:T(1024)S(1)}, f32[4096]{0:T(1024)}, u32[]{:S(2)}) copy-start(f32[4096]{0:T(1024)} %param.23) | copy-start | bytes 49156

commit v10 on v8

--- a/solution.py
+++ b/solution.py
@@ -317,8 +317,10 @@
         if not ready:
             load.wait()
             ready.append(1)
-        part[k] = jnp.dot(a, wo[...], preferred_element_type=F32)
-        hopb[k] = send(part.at[k, :, pl.ds(pl.multiple_of((1 - tp) * DY, DY), DY)], p_y.at[k], bs.at[k], br.at[k], over_y)
+        theirs, ours = (pl.ds(pl.multiple_of(t * DY, DY), DY) for t in (1 - tp, tp))
+        part[k, :, theirs] = jnp.dot(a, wo[:, theirs], preferred_element_type=F32)
+        hopb[k] = send(part.at[k, :, theirs], p_y.at[k], bs.at[k], br.at[k], over_y)
+        part[k, :, ours] = jnp.dot(a, wo[:, ours], preferred_element_type=F32)
 
     def piece(k, xx, yy, lo=0, width=DY):
         return (pl.ds(pl.multiple_of(k * CS + xx * R, R), R), pl.ds(pl.multiple_of(c * DC + yy * DY + lo, 128), width))
@@ -356,8 +358,8 @@
             cp.wait_send()
 
 
-def last_kernel(lens_hbm, kv, y_in, hid, bo_ref, held_in, k_part, v_part, ko_hbm, vo_hbm, out_hbm, held, lens, out, sem, osem):
-    load_lens = pltpu.make_async_copy(lens_hbm, lens, osem)
+def last_kernel(lens_hbm, kv, y_in, hid, bo_ref, held_in, k_part, v_part, ko_hbm, vo_hbm, out_hbm, held, lens, out, sem, osem, nsem):
+    load_lens = pltpu.make_async_copy(lens_hbm, lens, nsem)
     load_lens.start()
 
     def rows(i, _):
@@ -365,7 +367,15 @@
         out[r, :] = (hid[r, :].astype(F32) + y_in[r, :] + bo_ref[...]).astype(BF16)
         return 0
 
-    lax.fori_loop(0, B // 32, rows, 0, unroll=2)
+    half = B // 2
+    store_out = []
+
+    def finish_rows(e):
+        lax.fori_loop(e * (B // 32), (e + 1) * (B // 32), rows, 0, unroll=2)
+        store_out.append(pltpu.make_async_copy(out.at[pl.ds(e * half, half)], out_hbm.at[pl.ds(e * half, half)], osem.at[e]))
+        store_out[-1].start()
+
+    finish_rows(0)
     load_lens.wait()
     first = lax.axis_index("sq") * T
     n = B - AB
@@ -380,13 +390,10 @@
     put(64, 80)
     put(80, 96)
     put(96, 128)
-    lax.fori_loop(B // 32, B // 16, rows, 0, unroll=2)
-    store_out = pltpu.make_async_copy(out, out_hbm, osem)
-    store_out.start()
+    finish_rows(1)
     put(128, 192)
     put(192, 256)
-    store_out.wait()
-    for cp in copies:
+    for cp in store_out + copies:
         cp.wait()
 
 
@@ -442,7 +449,7 @@
             in_specs=[hbm, vm, vm, vm, vm, vm, hbm, hbm],
             out_specs=(hbm, hbm, hbm, vm),
             input_output_aliases={5: 3, 6: 0, 7: 1},
-            scratch_shapes=[pltpu.SMEM((B,), jnp.int32), pltpu.VMEM((B, D), BF16), sem((10,)), sem],
+            scratch_shapes=[pltpu.SMEM((B,), jnp.int32), pltpu.VMEM((B, D), BF16), sem((10,)), sem((2,)), sem],
             compiler_params=pltpu.CompilerParams(vmem_limit_bytes=6 * MIB),
             name="last",
         )(*far(cache_lens), *pin(kv, y), hidden, b_out[None], *pin(kv_held), k_part, v_part)

time: 72.4 us -> 72.3 us (level)
  no operation moved by 1% of the time
where the time goes in v10:
time: 72.3 us; the launch traced here: 72.2 us
  Pallas kernels  71.4 us (99%)
  between operations  0.86 us (1%)
    pallas_call x1, Pallas kernels, local_step(): pl.pallas_call(exchange_kernel, out_shape=(pltpu.VMEM((B, D), F32), held)...  47 us
    pallas_call x1, Pallas kernels, local_step(): pl.pallas_call(first_kernel, out_shape=(pltpu.VMEM((B * H, DH), F32), plt...  14.7 us
    pallas_call x1, Pallas kernels, local_step(): pl.pallas_call(last_kernel, out_shape=(cache, cache, jax.ShapeDtypeStruct...  9.68 us

profile of v10, /device:TPU:0, one launch (start us, length us, event | category | flops | bytes accessed | tf_op | source)
XLA Modules:
  0.0 72.2 jit_solution(651261806150096028)
XLA Ops:
  0.6 14.7 %first.1 = (f32[4096,128]{1,0:T(8,128)S(1)}, f32[512,128]{1,0:T(8,128)S(1)}, f32[1024,128]{1,0:T(8,128)S(1)}, f32[32,128]{1,0:T(8,128)S(1)}, bf16[256,256,128]{2...) custom-call(s32[256]{0:T(256)} %lens_hbm.5, bf16[256,4096]{1,0:T(8,128)(2,1)} %hid.1, bf16[256,256,128]{2,1,0:T(8,128)(2,1)} %k_hbm.3, ...), custom_call_target="tpu_custom_call" | custom-call | tf_op jit(solution)/shard_map/first/pallas_call | solution.py:414
  15.3 0.0 copy-start
  15.3 0.0 copy-start.1
  15.4 47.0 %exchange.1 = (f32[256,4096]{1,0:T(8,128)S(1)}, bf16[384,256,128]{2,1,0:T(8,128)(2,1)S(1)}) custom-call(s32[256]{0:T(256)} %lens_hbm.5, f32[4096,128]{1,0:T(8,128)S(1)} %get-tuple-element.15.q3, f32[512,128]{1,0:T(8,128)S(1)} %get-tuple-element.14.kv, f32[1024,128]{1,0:T(8,128)S(1)} %get-tuple-element.16.o_first, f32[32,128]{1,0:T(8,128)S(1)} %get-tuple-element.17.lse_first, ...), custom_call_target="tpu_custom_call" | custom-call | tf_op jit(solution)/shard_map/exchange/pallas_call | solution.py:428
  62.4 0.0 copy-done
  62.4 0.0 copy-done.1
  62.4 9.7 %last.1 = (bf16[256,256,128]{2,1,0:T(8,128)(2,1)}, bf16[256,256,128]{2,1,0:T(8,128)(2,1)}, bf16[256,4096]{1,0:T(8,128)(2,1)}, bf16[384,256,128]{2,1,0:T(8,128)(2,1)S(1)}) custom-call(s32[256]{0:T(256)} %lens_hbm.5, f32[512,128]{1,0:T(8,128)S(1)} %get-tuple-element.14.kv, ...), custom_call_target="tpu_custom_call", output_to_operand_aliasing={{3}: (5, {}), {0}: (6, {}), {1}: (7, {})} | custom-call | tf_op jit(solution)/shard_map/last/pallas_call | solution.py:446
Async XLA Ops:
  15.3 47.0 %copy-start = (bf16[256,4096]{1,0:T(8,128)(2,1)S(1)}, bf16[256,4096]{1,0:T(8,128)(2,1)}, u32[]{:S(2)}) copy-start(bf16[256,4096]{1,0:T(8,128)(2,1)} %hid.1) | copy-start | bytes 6291460
  15.3 47.0 %copy-start.1 = (f32[4096]{0:T(1024)S(1)}, f32[4096]{0:T(1024)}, u32[]{:S(2)}) copy-start(f32[4096]{0:T(1024)} %param.23) | copy-start | bytes 49156

commit v11 on v10

--- a/solution.py
+++ b/solution.py
@@ -31,7 +31,7 @@
 MIB = 1024 * 1024
 VIA_Y = 128
 SCHEDULE = [(s[0], int(s[1])) for s in (
-    "s0", "s1", "m0", "a2", "m1", "s2", "s3", "a4", "s4", "s5", "m2", "m3", "q0", "m4", "q1", "m5", "p0", "p1", "q2", "a6", "f0", "q3", "s6", "s7", "q4", "f1", "p2", "m6", "m7", "p3", "r0", "p4", "f2", "q5", "q6", "q7", "f3", "r1", "p5", "f4", "r2", "p6", "l0", "l1", "r3", "p7", "f5", "r4", "f6", "f7", "l2", "r5", "l3", "l4", "r6", "r7", "l5", "l6", "l7")]
+    "s0", "s1", "m0", "a2", "s2", "s3", "m1", "a4", "s4", "s5", "m2", "q0", "m3", "q1", "m4", "m5", "p0", "p1", "q2", "a6", "s6", "s7", "f0", "f1", "q3", "p2", "m6", "m7", "q4", "p3", "r0", "r1", "p4", "f2", "q5", "q6", "q7", "f3", "p5", "l0", "l1", "f4", "p6", "r2", "r3", "p7", "f5", "r4", "f6", "f7", "r5", "l2", "l4", "r6", "r7", "l3", "l5", "l6", "l7")]
 
 def attention_stages(lens, first, q3, kbuf, vbuf, base, vbase, kv, o_ref, lse_ref, bufs):
     lane = lax.broadcasted_iota(jnp.int32, (H, DH), 1)

time: 72.3 us -> 72.1 us (level)
  no operation moved by 1% of the time
where the time goes in v11:
time: 72.1 us; the launch traced here: 72 us
  Pallas kernels  71.2 us (99%)
  between operations  0.86 us (1%)
    pallas_call x1, Pallas kernels, local_step(): pl.pallas_call(exchange_kernel, out_shape=(pltpu.VMEM((B, D), F32), held)...  46.8 us
    pallas_call x1, Pallas kernels, local_step(): pl.pallas_call(first_kernel, out_shape=(pltpu.VMEM((B * H, DH), F32), plt...  14.7 us
    pallas_call x1, Pallas kernels, local_step(): pl.pallas_call(last_kernel, out_shape=(cache, cache, jax.ShapeDtypeStruct...  9.68 us

profile of v11, /device:TPU:0, one launch (start us, length us, event | category | flops | bytes accessed | tf_op | source)
XLA Modules:
  0.0 72.0 jit_solution(235398277997907059)
XLA Ops:
  0.6 14.7 %first.1 = (f32[4096,128]{1,0:T(8,128)S(1)}, f32[512,128]{1,0:T(8,128)S(1)}, f32[1024,128]{1,0:T(8,128)S(1)}, f32[32,128]{1,0:T(8,128)S(1)}, bf16[256,256,128]{2...) custom-call(s32[256]{0:T(256)} %lens_hbm.5, bf16[256,4096]{1,0:T(8,128)(2,1)} %hid.1, bf16[256,256,128]{2,1,0:T(8,128)(2,1)} %k_hbm.3, ...), custom_call_target="tpu_custom_call" | custom-call | tf_op jit(solution)/shard_map/first/pallas_call | solution.py:414
  15.3 0.0 copy-start
  15.3 0.0 copy-start.1
  15.4 46.8 %exchange.1 = (f32[256,4096]{1,0:T(8,128)S(1)}, bf16[384,256,128]{2,1,0:T(8,128)(2,1)S(1)}) custom-call(s32[256]{0:T(256)} %lens_hbm.5, f32[4096,128]{1,0:T(8,128)S(1)} %get-tuple-element.15.q3, f32[512,128]{1,0:T(8,128)S(1)} %get-tuple-element.14.kv, f32[1024,128]{1,0:T(8,128)S(1)} %get-tuple-element.16.o_first, f32[32,128]{1,0:T(8,128)S(1)} %get-tuple-element.17.lse_first, ...), custom_call_target="tpu_custom_call" | custom-call | tf_op jit(solution)/shard_map/exchange/pallas_call | solution.py:428
  62.2 0.0 copy-done
  62.2 0.0 copy-done.1
  62.2 9.7 %last.1 = (bf16[256,256,128]{2,1,0:T(8,128)(2,1)}, bf16[256,256,128]{2,1,0:T(8,128)(2,1)}, bf16[256,4096]{1,0:T(8,128)(2,1)}, bf16[384,256,128]{2,1,0:T(8,128)(2,1)S(1)}) custom-call(s32[256]{0:T(256)} %lens_hbm.5, f32[512,128]{1,0:T(8,128)S(1)} %get-tuple-element.14.kv, ...), custom_call_target="tpu_custom_call", output_to_operand_aliasing={{3}: (5, {}), {0}: (6, {}), {1}: (7, {})} | custom-call | tf_op jit(solution)/shard_map/last/pallas_call | solution.py:446
Async XLA Ops:
  15.3 46.8 %copy-start = (bf16[256,4096]{1,0:T(8,128)(2,1)S(1)}, bf16[256,4096]{1,0:T(8,128)(2,1)}, u32[]{:S(2)}) copy-start(bf16[256,4096]{1,0:T(8,128)(2,1)} %hid.1) | copy-start | bytes 6291460
  15.3 46.8 %copy-start.1 = (f32[4096]{0:T(1024)S(1)}, f32[4096]{0:T(1024)}, u32[]{:S(2)}) copy-start(f32[4096]{0:T(1024)} %param.23) | copy-start | bytes 49156
